TPU v7x, 256 devices: a whole 4x4x8 slice. The times are simulated.
256 devices in a mesh: gx: 32 (over z, x_lo, core), gy: 8 (over x_hi, y).
Axes of the slice: x: 4 (x_hi: 2, x_lo: 2; x = x_hi * 2 + x_lo), y: 4, z: 8, core: 2. Of those that a mesh axis runs over, the one named last changes fastest.
Arguments:
- volt: float32 [256, 512, 2048], P('gx', 'gy'), may hold values from -6 to 6
- drive: float32 [256, 512, 2048], P('gx', 'gy'), may hold values from -6 to 6
- region: int32 [256, 512, 32], P('gx', 'gy'), may hold values from 0 to 7
- diode_mask: int32 [256, 512, 32], P('gx', 'gy'), may hold values 0 or 1
- sigma_table: float32 [8], replicated, may hold values from 0.3 to 3
- cap_table: float32 [8], replicated, may hold values from 0.1 to 1
Outputs:
- residual: float32 [256, 512, 2048], P('gx', 'gy')
- coef_norms: float32 [64], replicated
All inputs are finite; a program needn't handle non-finite values. No bound on the sum of `diode_mask` on one device may be relied on, other than what follows from the above.
Results may differ from a plain program's by a relative error of at most 0.0003.
Values sent between devices are 32-bit elements; how exact they have to be, the bound alone decides.
No kernel may reach another device: no remote copies, remote signals or barrier semaphores. Data moves between devices by JAX's collectives and lax.ppermute only.
A program may use at most 192 MiB of HBM per device.

v0:
```python
import functools
import math

import jax
import jax.numpy as jnp
from jax import lax
from jax.sharding import Mesh
from jax.sharding import PartitionSpec as P

NZ = 32
H = 32
KC = 64
S = 256
GX = ("gx_0", "gx_1", "gx_2")
GY = ("gy_0", "gy_1")
GX_GY = ("gx_0", "gx_1", "gx_2", "gy_0", "gy_1")


base_freq = 0.1
norm_eps = 1e-06


def padded_2(block, sides, width, periodic):
    for axis, dim in sides:
        count = lax.axis_size(axis)
        forward = [(i, i + 1) for i in range(count - 1)]
        if periodic:
            forward.append((count - 1, 0))
        backward = [(target, source) for source, target in forward]
        low = lax.ppermute(
            lax.slice_in_dim(block, block.shape[dim] - width, None, axis=dim), axis, forward
        )
        high = lax.ppermute(lax.slice_in_dim(block, 0, width, axis=dim), axis, backward)
        block = jnp.concatenate([low, block, high], axis=dim)
    return block


def over_axes(array, axes):
    return functools.reduce(lax.psum, axes, array)


def cut_slab(array, first_idx, last_idx, along):
    return lax.slice_in_dim(array, first_idx, last_idx, axis=along)


def harmonic_mean(left, right):
    return 2.0 * left * right / (left + right)


def open_terms(volt_field, conduct, along):
    cell_count = volt_field.shape[along]
    widths = [(0, 0)] * volt_field.ndim
    widths[along] = (1, 1)
    padded_volt = jnp.pad(volt_field, widths)
    padded_cond = jnp.pad(conduct, widths)
    face_flux = harmonic_mean(
        cut_slab(padded_cond, 0, cell_count + 1, along),
        cut_slab(padded_cond, 1, cell_count + 2, along),
    ) * (
        cut_slab(padded_volt, 1, cell_count + 2, along)
        - cut_slab(padded_volt, 0, cell_count + 1, along)
    )
    return cut_slab(face_flux, 0, cell_count, along) - cut_slab(face_flux, 1, cell_count + 1, along)


def time_derivative(coefs):
    half_count = coefs.shape[-1] // 2
    orders = base_freq * jnp.arange(1, half_count + 1, dtype=jnp.float32)
    return jnp.concatenate(
        [orders * coefs[..., half_count:], -orders * coefs[..., :half_count]], axis=-1
    )


def spectral_tables(harmonics, samples):
    orders = jnp.arange(1, harmonics + 1, dtype=jnp.float32)
    times = 2.0 * math.pi * jnp.arange(samples, dtype=jnp.float32) / samples
    angles = orders[:, None] * times[None, :]
    synthesis = jnp.concatenate([jnp.cos(angles), jnp.sin(angles)], axis=0)
    analysis = synthesis.T * (2.0 / samples)
    return (synthesis, analysis)


def nonlinear_row(volt_row, diode_row, synthesis, analysis):
    coef_count = volt_row.shape[-1]
    flat = volt_row.reshape(-1, coef_count)
    cell_count = flat.shape[0]
    samples = jnp.dot(
        flat, synthesis, precision=lax.Precision.HIGHEST, preferred_element_type=jnp.float32
    )
    current = jax.nn.softplus(2.0 * samples) * 0.5
    charge = jnp.tanh(samples) * 0.5
    projected = jnp.dot(
        jnp.concatenate([current, charge], axis=0),
        analysis,
        precision=lax.Precision.HIGHEST,
        preferred_element_type=jnp.float32,
    )
    combined = projected[:cell_count] + time_derivative(projected[cell_count:])
    return combined.reshape(volt_row.shape) * diode_row[..., None]


def lookup(region, region_table):
    onehot = (region[..., None] == jnp.arange(region_table.shape[0], dtype=jnp.int32)).astype(
        jnp.float32
    )
    return jnp.sum(onehot * region_table, axis=-1)


def unpack(packed_block):
    row_width = NZ * KC
    volt_part = packed_block[..., :row_width].reshape(packed_block.shape[:-1] + (NZ, KC))
    cond_part = packed_block[..., row_width : row_width + NZ][..., None]
    return (volt_part, cond_part)


def edge_flux(low_block, high_block):
    low_volt, low_cond = unpack(low_block)
    high_volt, high_cond = unpack(high_block)
    return harmonic_mean(low_cond, high_cond) * (high_volt - low_volt)


def face_terms_both(padded, along, cell_count):
    face_flux = edge_flux(
        cut_slab(padded, 0, cell_count + 1, along), cut_slab(padded, 1, cell_count + 2, along)
    )
    return cut_slab(face_flux, 0, cell_count, along) - cut_slab(face_flux, 1, cell_count + 1, along)


def body(volt, drive, region, diode_mask, sigma_table, cap_table):
    rows_local, cols_local, row_width = volt.shape
    conduct = lookup(region, sigma_table)
    capacity = lookup(region, cap_table)[..., None]
    padding = jnp.zeros((rows_local, cols_local, 128 - NZ), jnp.float32)
    packed = jnp.concatenate([volt, conduct, padding], axis=2)
    volt_field = volt.reshape(rows_local, cols_local, NZ, KC)
    padded_rows = padded_2(packed, ((GX, 0),), 1, True)
    row_terms = face_terms_both(padded_rows, 0, rows_local)
    padded_cols = padded_2(packed, ((GY, 1),), 1, False)
    col_terms = face_terms_both(padded_cols, 1, cols_local)
    depth_terms = open_terms(volt_field, conduct[..., None], 2)
    synthesis, analysis = spectral_tables(H, S)
    diode_field = diode_mask.astype(jnp.float32)

    def diode_rows(pair):
        return nonlinear_row(pair[0], pair[1], synthesis, analysis)

    diode_part = lax.map(diode_rows, (volt_field, diode_field))
    drive_field = drive.reshape(rows_local, cols_local, NZ, KC)
    residual = (
        row_terms
        + col_terms
        + depth_terms
        + capacity * time_derivative(volt_field)
        + diode_part
        - drive_field
    )
    partial_value = jnp.sum(residual * residual, axis=(0, 1, 2))
    summed = over_axes(partial_value, GX_GY)
    cells_total = rows_local * cols_local * NZ * lax.axis_size(GX) * lax.axis_size(GY)
    norms_out = jnp.sqrt(summed / cells_total + norm_eps)
    return (residual.reshape(rows_local, cols_local, row_width), norms_out)


def solution(mesh):
    finer = Mesh(mesh.devices.reshape(8, 2, 2, 2, 4), ("gx_0", "gx_1", "gx_2", "gy_0", "gy_1"))
    in_specs = (P(GX, GY, None), P(GX, GY, None), P(GX, GY, None), P(GX, GY, None), P(), P())
    out_specs = (P(GX, GY, None), P())
    return jax.shard_map(body, mesh=finer, in_specs=in_specs, out_specs=out_specs, check_vma=False)
```

profile of v0, /device:TPU:1, one launch (start us, length us, event | category | flops | bytes accessed | tf_op | source)
XLA Modules:
  0.0 278.5 jit_solution(14886055668205441552)
XLA Ops:
  0.6 1.6 select_reduce_fusion
  2.4 5.9 %concatenate.29 = f32[8,64,2176]{2,1,0:T(8,128)} concatenate(f32[8,64,2048]{2,1,0:T(8,128)} %param.8, f32[8,64,32]{2,1,0:T(8,128)S(1)} %copy.52, f32[8,64,96]{2,1,0:T(8,128)S(1)} %broadcast_in_dim.7), dimensions={2} | concatenate | bytes 8912896 | tf_op jit(solution)/shard_map/concatenate | solution.py:134
  8.3 2.3 fusion.18
  10.7 2.6 collective-permute-start
  13.9 1.3 fusion.19
  15.2 2.6 collective-permute-start.2
  17.8 1.5 collective-permute-start.3
  19.3 7.8 %reshape.76 = f32[8,64,32,64]{3,2,1,0:T(8,128)} reshape(f32[8,64,2048]{2,1,0:T(8,128)} %param.8) | data formatting | bytes 8388608 | tf_op jit(solution)/shard_map/reshape | solution.py:135
  28.8 90.9 %while.10 = (s32[]{:T(128)}, f32[8,64,32,64]{3,2,1,0:T(8,128)}, f32[8,64,32,64]{3,2,1,0:T(8,128)}, f32[64,256]{1,0:T(8,128)}, f32[256,64]{1,0:T(8,128)S(1)}, /*index=5*/f32[8,64,32]{2,1,0:T(8,128)S(1)}, s32[]{:T(128)}) while((s32[]{:T(128)}, f32[8,64,32,64]{3,2,1,0:T(8,128)}, f32[8,64,32,64]{3,2,1,0:T(8,128)}, f32[64,256]{1,0:T(8,128)}, ...), condition=%wide.region_3.4_spmd, body=%wide.region_2.3_spmd.sunk | while | flops 1214251136 | bytes 16409685 | solution.py:147
  30.1 3.9 %fusion.33 = (f32[2048,256]{1,0:T(8,128)S(1)}, f32[2048,256]{1,0:T(8,128)S(1)}) fusion(f32[2048,64]{1,0:T(8,128)S(1)} %bitcast.31, f32[64,256]{1,0:T(8,128)} %get-tuple-element.147), kind=kOutput, calls=%fused_computation.5.clone.1 | convolution fusion | flops 407371776 | bytes 4784128 | tf_op jit(solution)/shard_map/while/body/eval_jaxpr/dot_general | solution.py:87
  34.0 4.2 %fusion.34 = f32[4096,64]{0,1:T(8,128)S(1)} fusion(f32[256,64]{1,0:T(8,128)S(1)} %get-tuple-element.148, f32[2048,256]{1,0:T(8,128)S(1)} %get-tuple-element.124, f32[2048,256]{1,0:T(8,128)S(1)} %get-tuple-element.125), kind=kOutput, calls=%fused_computation.1.clone.1 | convolution fusion | flops 806354944 | bytes 5308416 | tf_op jit(solution)/shard_map/while/body/eval_jaxpr/dot_general | solution.py:92
  38.8 1.4 multiply_dynamic-update-slice_fusion.2
  41.5 3.9 %fusion.33 = (f32[2048,256]{1,0:T(8,128)S(1)}, f32[2048,256]{1,0:T(8,128)S(1)}) fusion(f32[2048,64]{1,0:T(8,128)S(1)} %bitcast.31, f32[64,256]{1,0:T(8,128)} %get-tuple-element.147), kind=kOutput, calls=%fused_computation.5.clone.1 | convolution fusion | flops 407371776 | bytes 4784128 | tf_op jit(solution)/shard_map/while/body/eval_jaxpr/dot_general | solution.py:87
  45.4 4.2 %fusion.34 = f32[4096,64]{0,1:T(8,128)S(1)} fusion(f32[256,64]{1,0:T(8,128)S(1)} %get-tuple-element.148, f32[2048,256]{1,0:T(8,128)S(1)} %get-tuple-element.124, f32[2048,256]{1,0:T(8,128)S(1)} %get-tuple-element.125), kind=kOutput, calls=%fused_computation.1.clone.1 | convolution fusion | flops 806354944 | bytes 5308416 | tf_op jit(solution)/shard_map/while/body/eval_jaxpr/dot_general | solution.py:92
  50.2 1.3 multiply_dynamic-update-slice_fusion.2
  52.9 3.9 %fusion.33 = (f32[2048,256]{1,0:T(8,128)S(1)}, f32[2048,256]{1,0:T(8,128)S(1)}) fusion(f32[2048,64]{1,0:T(8,128)S(1)} %bitcast.31, f32[64,256]{1,0:T(8,128)} %get-tuple-element.147), kind=kOutput, calls=%fused_computation.5.clone.1 | convolution fusion | flops 407371776 | bytes 4784128 | tf_op jit(solution)/shard_map/while/body/eval_jaxpr/dot_general | solution.py:87
  56.8 4.2 %fusion.34 = f32[4096,64]{0,1:T(8,128)S(1)} fusion(f32[256,64]{1,0:T(8,128)S(1)} %get-tuple-element.148, f32[2048,256]{1,0:T(8,128)S(1)} %get-tuple-element.124, f32[2048,256]{1,0:T(8,128)S(1)} %get-tuple-element.125), kind=kOutput, calls=%fused_computation.1.clone.1 | convolution fusion | flops 806354944 | bytes 5308416 | tf_op jit(solution)/shard_map/while/body/eval_jaxpr/dot_general | solution.py:92
  64.2 3.9 %fusion.33 = (f32[2048,256]{1,0:T(8,128)S(1)}, f32[2048,256]{1,0:T(8,128)S(1)}) fusion(f32[2048,64]{1,0:T(8,128)S(1)} %bitcast.31, f32[64,256]{1,0:T(8,128)} %get-tuple-element.147), kind=kOutput, calls=%fused_computation.5.clone.1 | convolution fusion | flops 407371776 | bytes 4784128 | tf_op jit(solution)/shard_map/while/body/eval_jaxpr/dot_general | solution.py:87
  68.1 4.2 %fusion.34 = f32[4096,64]{0,1:T(8,128)S(1)} fusion(f32[256,64]{1,0:T(8,128)S(1)} %get-tuple-element.148, f32[2048,256]{1,0:T(8,128)S(1)} %get-tuple-element.124, f32[2048,256]{1,0:T(8,128)S(1)} %get-tuple-element.125), kind=kOutput, calls=%fused_computation.1.clone.1 | convolution fusion | flops 806354944 | bytes 5308416 | tf_op jit(solution)/shard_map/while/body/eval_jaxpr/dot_general | solution.py:92
  72.9 1.3 multiply_dynamic-update-slice_fusion.2
  75.5 3.9 %fusion.33 = (f32[2048,256]{1,0:T(8,128)S(1)}, f32[2048,256]{1,0:T(8,128)S(1)}) fusion(f32[2048,64]{1,0:T(8,128)S(1)} %bitcast.31, f32[64,256]{1,0:T(8,128)} %get-tuple-element.147), kind=kOutput, calls=%fused_computation.5.clone.1 | convolution fusion | flops 407371776 | bytes 4784128 | tf_op jit(solution)/shard_map/while/body/eval_jaxpr/dot_general | solution.py:87
  79.5 4.2 %fusion.34 = f32[4096,64]{0,1:T(8,128)S(1)} fusion(f32[256,64]{1,0:T(8,128)S(1)} %get-tuple-element.148, f32[2048,256]{1,0:T(8,128)S(1)} %get-tuple-element.124, f32[2048,256]{1,0:T(8,128)S(1)} %get-tuple-element.125), kind=kOutput, calls=%fused_computation.1.clone.1 | convolution fusion | flops 806354944 | bytes 5308416 | tf_op jit(solution)/shard_map/while/body/eval_jaxpr/dot_general | solution.py:92
  84.3 1.3 multiply_dynamic-update-slice_fusion.2
  86.9 3.9 %fusion.33 = (f32[2048,256]{1,0:T(8,128)S(1)}, f32[2048,256]{1,0:T(8,128)S(1)}) fusion(f32[2048,64]{1,0:T(8,128)S(1)} %bitcast.31, f32[64,256]{1,0:T(8,128)} %get-tuple-element.147), kind=kOutput, calls=%fused_computation.5.clone.1 | convolution fusion | flops 407371776 | bytes 4784128 | tf_op jit(solution)/shard_map/while/body/eval_jaxpr/dot_general | solution.py:87
  90.8 4.2 %fusion.34 = f32[4096,64]{0,1:T(8,128)S(1)} fusion(f32[256,64]{1,0:T(8,128)S(1)} %get-tuple-element.148, f32[2048,256]{1,0:T(8,128)S(1)} %get-tuple-element.124, f32[2048,256]{1,0:T(8,128)S(1)} %get-tuple-element.125), kind=kOutput, calls=%fused_computation.1.clone.1 | convolution fusion | flops 806354944 | bytes 5308416 | tf_op jit(solution)/shard_map/while/body/eval_jaxpr/dot_general | solution.py:92
  95.6 1.3 multiply_dynamic-update-slice_fusion.2
  98.2 3.9 %fusion.33 = (f32[2048,256]{1,0:T(8,128)S(1)}, f32[2048,256]{1,0:T(8,128)S(1)}) fusion(f32[2048,64]{1,0:T(8,128)S(1)} %bitcast.31, f32[64,256]{1,0:T(8,128)} %get-tuple-element.147), kind=kOutput, calls=%fused_computation.5.clone.1 | convolution fusion | flops 407371776 | bytes 4784128 | tf_op jit(solution)/shard_map/while/body/eval_jaxpr/dot_general | solution.py:87
  102.2 4.2 %fusion.34 = f32[4096,64]{0,1:T(8,128)S(1)} fusion(f32[256,64]{1,0:T(8,128)S(1)} %get-tuple-element.148, f32[2048,256]{1,0:T(8,128)S(1)} %get-tuple-element.124, f32[2048,256]{1,0:T(8,128)S(1)} %get-tuple-element.125), kind=kOutput, calls=%fused_computation.1.clone.1 | convolution fusion | flops 806354944 | bytes 5308416 | tf_op jit(solution)/shard_map/while/body/eval_jaxpr/dot_general | solution.py:92
  107.0 1.4 multiply_dynamic-update-slice_fusion.2
  109.6 3.9 %fusion.33 = (f32[2048,256]{1,0:T(8,128)S(1)}, f32[2048,256]{1,0:T(8,128)S(1)}) fusion(f32[2048,64]{1,0:T(8,128)S(1)} %bitcast.31, f32[64,256]{1,0:T(8,128)} %get-tuple-element.147), kind=kOutput, calls=%fused_computation.5.clone.1 | convolution fusion | flops 407371776 | bytes 4784128 | tf_op jit(solution)/shard_map/while/body/eval_jaxpr/dot_general | solution.py:87
  113.5 4.2 %fusion.34 = f32[4096,64]{0,1:T(8,128)S(1)} fusion(f32[256,64]{1,0:T(8,128)S(1)} %get-tuple-element.148, f32[2048,256]{1,0:T(8,128)S(1)} %get-tuple-element.124, f32[2048,256]{1,0:T(8,128)S(1)} %get-tuple-element.125), kind=kOutput, calls=%fused_computation.1.clone.1 | convolution fusion | flops 806354944 | bytes 5308416 | tf_op jit(solution)/shard_map/while/body/eval_jaxpr/dot_general | solution.py:92
  118.3 1.3 multiply_dynamic-update-slice_fusion.2
  119.9 13.0 %slice_multiply_fusion.3 = (f32[8,64,32,32]{3,2,1,0:T(8,128)}, f32[8,64,32,32]{3,2,1,0:T(8,128)}) fusion(f32[8,64,32,64]{3,2,1,0:T(8,128)} %get-tuple-element.151, f32[32]{0:T(128)S(1)} %get-tuple-element.79, f32[32]{0:T(128)} %get-tuple-element.80), kind=kLoop, calls=%fused_computation.21 | loop fusion | flops 1048576 | bytes 8388864 | tf_op jit(solution)/shard_map/mul | solution.py:70
  132.9 6.8 %fusion.8 = f32[8,64,33,64]{3,2,1,0:T(8,128)} fusion(f32[8,64,32,64]{3,2,1,0:T(8,128)S(1)} %copy-done, f32[8,64,33]{2,1,0:T(8,128)S(1)} %copy.59), kind=kLoop, calls=%fused_computation.19 | loop fusion | flops 2162688 | bytes 8587264 | tf_op jit(solution)/shard_map/mul | solution.py:56
  139.8 7.8 %reshape.77 = f32[8,64,32,64]{3,2,1,0:T(8,128)} reshape(f32[8,64,2048]{2,1,0:T(8,128)} %param.9) | data formatting | bytes 8388608 | tf_op jit(solution)/shard_map/reshape | solution.py:148
  148.8 7.3 %fusion.14 = f32[8,65,2048]{2,1,0:T(8,128)} fusion(f32[8,64,2176]{2,1,0:T(8,128)} %concatenate.29, f32[8,1,2176]{2,1,0:T(1,128)S(1)} %copy.54, f32[8,1,2176]{2,1,0:T(1,128)S(1)} %copy.56), kind=kLoop, calls=%fused_computation.33 | loop fusion | flops 3194880 | bytes 8855552 | tf_op jit(solution)/shard_map/sub | solution.py:119
  156.2 7.6 %reshape.79 = f32[8,65,32,64]{3,2,1,0:T(8,128)} reshape(f32[8,65,2048]{2,1,0:T(8,128)} %fusion.14) | data formatting | bytes 8519680 | tf_op jit(solution)/shard_map/sub | solution.py:119
  163.9 8.4 %broadcast_multiply_fusion.1 = f32[8,65,32,64]{3,2,1,0:T(8,128)} fusion(f32[8,65,32,64]{3,2,1,0:T(8,128)} %reshape.79, f32[8,65,32]{2,1,0:T(8,128)S(1)} %add_divide_fusion), kind=kLoop, calls=%fused_computation.39 | loop fusion | flops 1064960 | bytes 8586240 | tf_op jit(solution)/shard_map/mul | solution.py:119
  172.3 2.8 fusion.15
  175.1 8.7 %sub.28 = f32[9,64,32,64]{3,2,1,0:T(8,128)} reshape(f32[9,64,2048]{2,1,0:T(8,128)} %fusion.15) | data formatting | bytes 9437184 | tf_op jit(solution)/shard_map/sub | solution.py:119
  185.0 8.7 %broadcast_multiply_fusion = f32[9,64,32,64]{3,2,1,0:T(8,128)} fusion(f32[9,64,32,64]{3,2,1,0:T(8,128)} %sub.28, f32[9,64,32]{2,1,0:T(8,128)S(1)} %add_divide_fusion.1), kind=kLoop, calls=%fused_computation.38 | loop fusion | flops 1179648 | bytes 9510912 | tf_op jit(solution)/shard_map/mul | solution.py:119
  193.7 31.9 %multiply_reduce_fusion = (f32[64]{0:T(128)S(1)}, f32[8,64,32,64]{3,2,1,0:T(8,128)}) fusion(f32[8,64,32,64]{3,2,1,0:T(8,128)} %reshape.77, f32[8,64,32,64]{3,2,1,0:T(8,128)} %get-tuple-element.34, f32[8,64,32,32]{3,2,1,0:T(8,128)} %get-tuple-element.70, f32[8,64,32,32]{3,2,1,0:T(8,128)} %get-tuple-element.69, f32[8,64,32]{2,1,0:T(8,128)S(1)} %copy.60, ...), kind=kLoop, calls=%fused_computation.31 | loop fusion | flops 12582848 | bytes 42008832 | tf_op jit(solution)/shard_map/reduce_sum | solution.py:157
  225.6 7.8 %reshape.78 = f32[8,64,2048]{2,1,0:T(8,128)} reshape(f32[8,64,32,64]{3,2,1,0:T(8,128)} %get-tuple-element.62) | data formatting | bytes 8388608 | tf_op jit(solution)/shard_map/reshape | solution.py:161
  233.4 16.2 %psum.35 = f32[64]{0:T(128)S(1)} all-reduce(f32[64]{0:T(128)S(1)} %get-tuple-element.61), channel_id=1, replica_groups=mesh['gx_0'=8,'gx_1'=2,'gx_2'=2,'gy_0'=2,'gy_1'=4] {'gx_0'}, use_global_device_ids=true, to_apply=%region_5.6 | all-reduce | flops 64 | bytes 512 | tf_op jit(solution)/shard_map/psum | solution.py:39
  249.7 3.8 %psum.36 = f32[64]{0:T(128)S(1)} all-reduce(f32[64]{0:T(128)S(1)} %psum.35), channel_id=1, replica_groups=mesh['gx_0'=8,'gx_1'=2,'gx_2'=2,'gy_0'=2,'gy_1'=4] {'gx_1'}, use_global_device_ids=true, to_apply=%region_6.7 | all-reduce | flops 64 | bytes 512 | tf_op jit(solution)/shard_map/psum | solution.py:39
  253.4 8.8 %psum.37 = f32[64]{0:T(128)S(1)} all-reduce(f32[64]{0:T(128)S(1)} %psum.36), channel_id=1, replica_groups=mesh['gx_0'=8,'gx_1'=2,'gx_2'=2,'gy_0'=2,'gy_1'=4] {'gx_2'}, use_global_device_ids=true, to_apply=%region_7.8 | all-reduce | flops 64 | bytes 512 | tf_op jit(solution)/shard_map/psum | solution.py:39
  262.3 9.7 %psum.38 = f32[64]{0:T(128)S(1)} all-reduce(f32[64]{0:T(128)S(1)} %psum.37), channel_id=1, replica_groups=mesh['gx_0'=8,'gx_1'=2,'gx_2'=2,'gy_0'=2,'gy_1'=4] {'gy_0'}, use_global_device_ids=true, to_apply=%region_8.9 | all-reduce | flops 64 | bytes 512 | tf_op jit(solution)/shard_map/psum | solution.py:39
  272.0 6.0 %psum.39 = f32[64]{0:T(128)S(1)} all-reduce(f32[64]{0:T(128)S(1)} %psum.38), channel_id=1, replica_groups=mesh['gx_0'=8,'gx_1'=2,'gx_2'=2,'gy_0'=2,'gy_1'=4] {'gy_1'}, use_global_device_ids=true, to_apply=%region_9.10 | all-reduce | flops 64 | bytes 512 | tf_op jit(solution)/shard_map/psum | solution.py:39
  (89 shorter events, 21.5 us)
Async XLA Ops:
  8.3 20.3 %copy-start.1 = (s32[8,64,32]{1,2,0:T(8,128)S(1)}, s32[8,64,32]{1,2,0:T(8,128)}, u32[]{:S(2)}) copy-start(s32[8,64,32]{1,2,0:T(8,128)} %param.11) | copy-start | bytes 196612
  10.7 161.6 %collective-permute-start = (f32[1,64,2176]{2,1,0:T(8,128)}, f32[1,64,2176]{2,1,0:T(8,128)S(1)}, u32[]{:S(2)}, u32[]{:S(2)}) collective-permute-start(f32[1,64,2176]{2,1,0:T(8,128)} %get-tuple-element.72), channel_id=1, source_target_pairs={{0,8},{8,16},{16,24},{24,32},{32,40},{40,48},{48,56},{56,64},{64,7... | collective-permute-start | bytes 1671176 | tf_op jit(solution)/shard_map/ppermute | solution.py:30
  13.3 159.0 %collective-permute-start.1 = (f32[1,64,2176]{2,1,0:T(8,128)}, f32[1,64,2176]{2,1,0:T(8,128)S(1)}, u32[]{:S(2)}, u32[]{:S(2)}) collective-permute-start(f32[1,64,2176]{2,1,0:T(8,128)} %get-tuple-element.71), channel_id=1, source_target_pairs={{8,0},{16,8},{24,16},{32,24},{40,32},{48,40},{56,48},{64,56},{72,6... | collective-permute-start | bytes 1671176 | tf_op jit(solution)/shard_map/ppermute | solution.py:33
  15.2 132.4 %collective-permute-start.2 = (f32[8,1,2176]{2,0,1:T(8,128)S(1)}, f32[8,1,2176]{2,0,1:T(8,128)S(1)}, u32[]{:S(2)}, u32[]{:S(2)}) collective-permute-start(f32[8,1,2176]{2,0,1:T(8,128)S(1)} %copy.53), channel_id=1, source_target_pairs={{0,1},{1,2},{2,3},{3,4},{4,5},{5,6},{6,7},{8,9},{9,10},{10,11},{11... | collective-permute-start | bytes 208904 | tf_op jit(solution)/shard_map/ppermute | solution.py:30
  17.8 129.9 %collective-permute-start.3 = (f32[8,1,2176]{2,0,1:T(8,128)S(1)}, f32[8,1,2176]{2,0,1:T(8,128)}, u32[]{:S(2)}, u32[]{:S(2)}) collective-permute-start(f32[8,1,2176]{2,0,1:T(8,128)S(1)} %copy.55), channel_id=1, source_target_pairs={{1,0},{2,1},{3,2},{4,3},{5,4},{6,5},{7,6},{9,8},{10,9},{11,10},{12... | collective-permute-start | bytes 208904 | tf_op jit(solution)/shard_map/ppermute | solution.py:33
  119.9 13.0 %copy-start = (f32[8,64,32,64]{3,2,1,0:T(8,128)S(1)}, f32[8,64,32,64]{3,2,1,0:T(8,128)}, u32[]{:S(2)}) copy-start(f32[8,64,32,64]{3,2,1,0:T(8,128)} %get-tuple-element.151) | copy-start | bytes 12582916
  147.6 8.5 %slice-start = ((s8[4456448]{0:T(1024)(128)(4,1)}), s8[4194304]{0:T(1024)(128)(4,1)S(1)}, s32[]{:S(2)}) async-start(s8[4456448]{0:T(1024)(128)(4,1)} %bitcast.26), calls=%async_computation | async-start | bytes 8388608
  148.8 7.3 %slice-start.1 = ((s8[4456448]{0:T(1024)(128)(4,1)}), s8[262144]{0:T(1024)(128)(4,1)S(1)}, s32[]{:S(2)}) async-start(s8[4456448]{0:T(1024)(128)(4,1)} %bitcast.26), calls=%async_computation.1 | async-start | bytes 524288
  156.2 16.1 %slice-start.2 = ((s8[4456448]{0:T(1024)(128)(4,1)}), s8[262144]{0:T(1024)(128)(4,1)S(1)}, s32[]{:S(2)}) async-start(s8[4456448]{0:T(1024)(128)(4,1)} %bitcast.28), calls=%async_computation.2 | async-start | bytes 524288
  163.9 8.4 %slice-start.3 = ((s8[4456448]{0:T(1024)(128)(4,1)}), s8[4194304]{0:T(1024)(128)(4,1)S(1)}, s32[]{:S(2)}) async-start(s8[4456448]{0:T(1024)(128)(4,1)} %bitcast.28), calls=%async_computation.3 | async-start | bytes 8388608
where the time goes:
time: 283 us; the launch traced here: 278 us
  other arithmetic  96 us (34%)
  matrix products  65.3 us (23%)
  local copies, waits for them, and re-layouts  64.3 us (23%)
  blocking collectives  44.5 us (16%)
  starting transfers between devices  7.27 us (3%)
    psum x5, blocking collectives, over_axes(): return functools.reduce(lax.psum, axes, array)  44.5 us
    dot_general x8, matrix products, nonlinear_row(): jnp.dot(jnp.concatenate([current, charge], axis=0), analysis, precision=l...  34 us
    reduce_sum x1, other arithmetic, body(): partial_value = jnp.sum(residual * residual, axis=(0, 1, 2))  31.9 us
    dot_general x8, matrix products, nonlinear_row(): jnp.dot(flat, synthesis, precision=lax.Precision.HIGHEST, preferred_eleme...  31.4 us
    mul x2, other arithmetic, edge_flux(): return harmonic_mean(low_cond, high_cond) * (high_volt - low_volt)  17.1 us
    sub x2, local copies, waits for them, and re-layouts, edge_flux(): return harmonic_mean(low_cond, high_cond) * (high_volt - low_volt)  16.4 us
    mul x9, other arithmetic, time_derivative(): orders * coefs[..., half_count:]  13.9 us
    dynamic_update_slice x8, other arithmetic, body(): diode_part = lax.map(diode_rows, (volt_field, diode_field))  10.7 us
  transfers between devices with their start and end apart: 4, of which 0 were waited for; matrix products, arithmetic and copies ran while one was open for 55% of the time, Pallas kernels for 0%

commit v1 on v0

v1 whole, which is shorter than its diff:
```python
import functools
import math

import jax
import jax.numpy as jnp
import numpy as np
from jax import lax
from jax.experimental import pallas as pl
from jax.experimental.pallas import tpu as pltpu
from jax.sharding import PartitionSpec as P

NZ = 32
H = 32
KC = 64
S = 256
REGIONS = 8
ROWS = 8
COLS = 64
PAIRS = NZ // 2
LANES = 128
GROUPS = ROWS * COLS // LANES
CELLS = ROWS * COLS

base_freq = 0.1
norm_eps = 1e-06

GX = 0
GYP = GX + GROUPS + 1
GYM = GYP + GROUPS
GYH = GYM + GROUPS
GZP = GYH + GROUPS
GZM = GZP + GROUPS
CAP = GZM + GROUPS
DIO = CAP + GROUPS
GSUM = DIO + GROUPS
FIELDS = GSUM + GROUPS


def halves(table):
    high = table.astype(jnp.bfloat16)
    low = (table - high.astype(np.float64)).astype(jnp.bfloat16)
    return high, low


def constant_tables():
    orders = np.arange(1, H + 1, dtype=np.float64)
    angles = orders[:, None] * (2.0 * math.pi * np.arange(S) / S)[None, :]
    cosines, sines = np.cos(angles), np.sin(angles)
    synthesis = np.concatenate([cosines, sines], axis=0)
    high, low = halves(synthesis.T)
    forward = np.concatenate([high, low, high, low], axis=1)
    scaled = base_freq * orders[:, None]
    from_even = synthesis / S
    from_odd = np.concatenate([scaled * sines, -scaled * cosines], axis=0) / S
    even_high, even_low = halves(from_even)
    odd_high, odd_low = halves(from_odd)
    backward = np.concatenate(
        [
            np.concatenate([even_high, even_high, odd_high, odd_high], axis=1),
            np.concatenate([even_low, even_low, odd_low, odd_low], axis=1),
        ],
        axis=0,
    )
    rates = np.concatenate([scaled, -scaled], axis=0).astype(np.float32)
    spread = np.zeros((16, CELLS), np.float32)
    for row in range(ROWS):
        group, half = row % GROUPS, row // GROUPS
        spread[row, group * LANES + half * COLS] = 1.0
        spread[ROWS + row, group * LANES + half * COLS + COLS - 1] = 1.0
    return forward, backward, rates, spread


def split(values):
    high = values.astype(jnp.bfloat16)
    low = (values - high.astype(jnp.float32)).astype(jnp.bfloat16)
    return high, low


def dot(left, right):
    return jnp.dot(left, right, preferred_element_type=jnp.float32)


def dot_exact(left, right):
    return jnp.dot(
        left, right, preferred_element_type=jnp.float32, precision=lax.Precision.HIGHEST
    )


def harmonic_mean(left, right):
    return 2.0 * left * right / (left + right)


def look_up(region, table_ref):
    found = jnp.full(region.shape, table_ref[0], jnp.float32)
    for index in range(1, REGIONS):
        found = jnp.where(region == float(index), table_ref[index], found)
    return found


def in_groups(block, group):
    return jnp.concatenate([block[group], block[group + GROUPS]], axis=0)


def fill_factors(sigma_ref, cap_ref, region_ref, mask_ref, row_region, col_region, spread, factors):
    lane = lax.broadcasted_iota(jnp.int32, (NZ, LANES), 1)
    first = lane < COLS
    column = jnp.where(first, lane, lane - COLS)
    region = [in_groups(region_ref, g).astype(jnp.float32).T for g in range(GROUPS)]
    conduct = [look_up(r, sigma_ref) for r in region]
    row_halo = look_up(row_region[...].T, sigma_ref)
    is_edge = (column == 0) | (column == COLS - 1)
    col_spread = dot_exact(col_region[...].T, spread)
    below = jnp.where(first, row_halo, pltpu.roll(conduct[GROUPS - 1], COLS, 1))
    above = jnp.where(first, pltpu.roll(conduct[0], COLS, 1), row_halo)
    stack = [below] + conduct + [above]
    faces = [harmonic_mean(stack[g], stack[g + 1]) for g in range(GROUPS + 1)]
    layer = lax.broadcasted_iota(jnp.int32, (NZ, LANES), 0)
    for g in range(GROUPS + 1):
        factors[GX + g] = faces[g]
    for g in range(GROUPS):
        here = conduct[g]
        plus = harmonic_mean(here, pltpu.roll(here, LANES - 1, 1))
        plus = jnp.where(column == COLS - 1, 0.0, plus)
        minus = harmonic_mean(here, pltpu.roll(here, 1, 1))
        minus = jnp.where(column == 0, 0.0, minus)
        outer = col_spread[:, g * LANES : (g + 1) * LANES]
        halo = jnp.where(is_edge, harmonic_mean(here, outer), 0.0)
        upper = harmonic_mean(here, pltpu.roll(here, NZ - 1, 0))
        upper = jnp.where(layer == NZ - 1, 0.0, upper)
        lower = harmonic_mean(here, pltpu.roll(here, 1, 0))
        lower = jnp.where(layer == 0, 0.0, lower)
        diode = in_groups(mask_ref, g).astype(jnp.float32).T
        factors[GYP + g] = plus
        factors[GYM + g] = minus
        factors[GYH + g] = halo
        factors[GZP + g] = upper
        factors[GZM + g] = lower
        factors[CAP + g] = look_up(region[g], cap_ref)
        factors[DIO + g] = diode
        factors[GSUM + g] = (
            faces[g] + faces[g + 1] + plus + minus + halo + upper + lower + 0.5 * diode
        )


def diode_terms(volt, forward, backward):
    high, low = split(volt)
    samples = dot(forward, jnp.concatenate([high, high, low, low], axis=0))
    odd = jnp.tanh(samples)
    even = jnp.abs(samples) - jnp.log(1.0 + jnp.abs(odd))
    spectrum = dot(backward, jnp.concatenate(split(even) + split(odd), axis=0))
    return spectrum[:KC] + spectrum[KC:]


def kernel(
    sigma_ref,
    cap_ref,
    volt_ref,
    drive_ref,
    region_ref,
    mask_ref,
    row_ref,
    col_ref,
    row_region,
    col_region,
    forward_ref,
    backward_ref,
    rates_ref,
    spread_ref,
    out_ref,
    squares_ref,
    turned,
    factors,
):
    step = pl.program_id(0)

    def turn():
        for g in range(GROUPS):
            turned[step, :, g * LANES : (g + 1) * LANES] = in_groups(volt_ref, g).T

    def residual():
        pair = step - 1
        before = jnp.maximum(pair - 1, 0)
        lane = lax.broadcasted_iota(jnp.int32, (KC, LANES), 1)
        first = lane < COLS
        row_halo = row_ref[...].T
        col_halo = dot_exact(col_ref[...].T, spread_ref[...])
        parts = [[] for _ in range(GROUPS)]
        for half in range(2):
            layer = 2 * pair + half
            mine = slice(half * KC, (half + 1) * KC)
            other = slice((1 - half) * KC, (2 - half) * KC)
            diode = diode_terms(turned[pair, mine, :], forward_ref[...], backward_ref[...])

            def factor(index):
                return factors[index, pl.ds(layer, 1), :]

            def group_of(which, rows, g):
                return turned[which, rows, g * LANES : (g + 1) * LANES]

            volts = [group_of(pair, mine, g) for g in range(GROUPS)]
            halo = row_halo[mine]
            below = jnp.where(first, halo, pltpu.roll(volts[GROUPS - 1], COLS, 1))
            above = jnp.where(first, pltpu.roll(volts[0], COLS, 1), halo)
            stack = [below] + volts + [above]
            for g in range(GROUPS):
                here = volts[g]
                down = group_of(before if half == 0 else pair, other, g)
                up = group_of(pair if half == 0 else pair + 1, other, g)
                edge = col_halo[mine, g * LANES : (g + 1) * LANES]
                swapped = jnp.concatenate([here[KC // 2 :], here[: KC // 2]], axis=0)
                total = factor(GSUM + g) * here
                total -= factor(GX + g) * stack[g]
                total -= factor(GX + g + 1) * stack[g + 2]
                total -= factor(GYP + g) * pltpu.roll(here, LANES - 1, 1)
                total -= factor(GYM + g) * pltpu.roll(here, 1, 1)
                total -= factor(GYH + g) * edge
                total -= factor(GZP + g) * up
                total -= factor(GZM + g) * down
                total += factor(CAP + g) * rates_ref[...] * swapped
                total += factor(DIO + g) * diode[:, g * LANES : (g + 1) * LANES]
                parts[g].append(total)
        squares = jnp.zeros((8, LANES), jnp.float32)
        for g in range(GROUPS):
            cells = jnp.concatenate(parts[g], axis=0).T
            for which in range(2):
                row = g + which * GROUPS
                value = cells[which * COLS : (which + 1) * COLS] - drive_ref[row]
                out_ref[row] = value
                squares += jnp.sum((value * value).reshape(COLS // 8, 8, LANES), axis=0)
        squares_ref[...] = jnp.where(step == 1, squares, squares_ref[...] + squares)

    @pl.when(step == 0)
    def _():
        fill_factors(
            sigma_ref, cap_ref, region_ref, mask_ref, row_region, col_region, spread_ref[...], factors
        )
        turn()

    @pl.when(step > 0)
    def _():
        turn()
        residual()


def local_residual(volt, drive, region, mask, rows, cols, sigma_table, cap_table):
    forward, backward, rates, spread = constant_tables()
    width = NZ * KC
    now = lambda s: jnp.minimum(s, PAIRS - 1)
    late = lambda s: jnp.maximum(s - 1, 0)
    whole = lambda *shape: pl.BlockSpec(shape, lambda s: (0,) * len(shape))
    smem = pl.BlockSpec(memory_space=pltpu.SMEM)
    samples = CELLS * NZ * S
    return pl.pallas_call(
        kernel,
        grid=(PAIRS + 1,),
        in_specs=[
            smem,
            smem,
            pl.BlockSpec((ROWS, COLS, LANES), lambda s: (0, 0, now(s))),
            pl.BlockSpec((ROWS, COLS, LANES), lambda s: (0, 0, late(s))),
            whole(ROWS, COLS, NZ),
            whole(ROWS, COLS, NZ),
            pl.BlockSpec((2 * COLS, LANES), lambda s: (0, late(s))),
            pl.BlockSpec((2 * ROWS, LANES), lambda s: (0, late(s))),
            whole(2 * COLS, NZ),
            whole(2 * ROWS, NZ),
            whole(*forward.shape),
            whole(*backward.shape),
            whole(*rates.shape),
            whole(*spread.shape),
        ],
        out_specs=[
            pl.BlockSpec((ROWS, COLS, LANES), lambda s: (0, 0, late(s))),
            whole(8, LANES),
        ],
        out_shape=[
            jax.ShapeDtypeStruct((ROWS, COLS, width), jnp.float32),
            jax.ShapeDtypeStruct((8, LANES), jnp.float32),
        ],
        scratch_shapes=[
            pltpu.VMEM((PAIRS + 1, LANES, CELLS), jnp.float32),
            pltpu.VMEM((FIELDS, NZ, LANES), jnp.float32),
        ],
        compiler_params=pltpu.CompilerParams(
            dimension_semantics=("arbitrary",), vmem_limit_bytes=48 * 1024 * 1024
        ),
        cost_estimate=pl.CostEstimate(
            flops=samples * 1000, bytes_accessed=3 * 4 * CELLS * width, transcendentals=2 * samples
        ),
        name="residual",
    )(
        sigma_table,
        cap_table,
        volt,
        drive,
        region,
        mask,
        rows[0],
        cols[0],
        rows[1],
        cols[1],
        jnp.asarray(forward),
        jnp.asarray(backward),
        jnp.asarray(rates),
        jnp.asarray(spread),
    )


def neighbours(volt, region, axis, dim, periodic):
    count = lax.axis_size(axis)
    forward = [(i, i + 1) for i in range(count - 1)]
    if periodic:
        forward.append((count - 1, 0))
    backward = [(target, source) for source, target in forward]
    extent = volt.shape[dim]

    def slab(index):
        cells = lax.index_in_dim(volt, index, dim, keepdims=False)
        kinds = lax.index_in_dim(region, index, dim, keepdims=False).astype(jnp.float32)
        return jnp.pad(jnp.concatenate([cells, kinds + 1.0], axis=1), ((0, 0), (0, LANES - NZ)))

    low = lax.ppermute(slab(extent - 1), axis, forward)
    high = lax.ppermute(slab(0), axis, backward)
    both = jnp.concatenate([low, high], axis=0)
    width = NZ * KC
    return both[:, :width], both[:, width : width + NZ]


def body(volt, drive, region, diode_mask, sigma_table, cap_table):
    row_volt, row_kind = neighbours(volt, region, "gx", 0, True)
    col_volt, col_kind = neighbours(volt, region, "gy", 1, False)
    kinds = jnp.arange(1, REGIONS + 1, dtype=jnp.float32)
    col_conduct = jnp.sum(
        jnp.where(col_kind[..., None] == kinds, sigma_table, 0.0), axis=-1
    )
    residual, squares = local_residual(
        volt,
        drive,
        region,
        diode_mask,
        (row_volt, row_kind - 1.0),
        (col_volt, col_conduct),
        sigma_table,
        cap_table,
    )
    partial = jnp.sum(squares.reshape(8, 2, KC), axis=(0, 1))
    summed = lax.psum(partial, ("gx", "gy"))
    cells_total = CELLS * NZ * lax.axis_size("gx") * lax.axis_size("gy")
    return residual, jnp.sqrt(summed / cells_total + norm_eps)


def solution(mesh):
    spec = P("gx", "gy", None)
    return jax.shard_map(
        body,
        mesh=mesh,
        in_specs=(spec, spec, spec, spec, P(), P()),
        out_specs=(spec, P()),
        check_vma=False,
    )
```

time: 283 us -> 139 us (0.49); the launches traced: 278 us -> 139 us
  other arithmetic: 96 us -> 0.8 us
  matrix products: 65.3 us -> 0 us
  local copies, waits for them, and re-layouts: 64.3 us -> 5.37 us
  blocking collectives: 44.5 us -> 82 us
  Pallas kernels: 0 us -> 27.6 us
  waiting for transfers between devices: 0.01 us -> 14.5 us
    dot_general x16 -> x0, matrix products: 65.3 us -> none  [the longest x8 34 us: nonlinear_row(): jnp.dot(jnp.concatenate([current, charge], axis=0), analysis, precision=l...]
    mul x23 -> x0, other arithmetic: 39.1 us -> none  [the longest x2 17.1 us: edge_flux(): return harmonic_mean(low_cond, high_cond) * (high_volt - low_volt)]
    psum x5 -> x1, blocking collectives: 44.5 us -> 82 us  [body(): summed = lax.psum(partial, ('gx', 'gy'))]
    reduce_sum x2 -> x3, other arithmetic: 33.6 us -> 0.13 us  [the longest x1 0.09 us: body(): jnp.sum(jnp.where(col_kind[..., None] == kinds, sigma_table, 0.0), axis=-1)]
    pallas_call x0 -> x1, Pallas kernels: none -> 27.6 us  [local_residual(): pl.pallas_call(kernel, grid=(PAIRS + 1,), in_specs=[smem, smem, pl.BlockS...]
    reshape x3 -> x0, local copies, waits for them, and re-layouts: 23.4 us -> none  [the longest x1 7.81 us: body(): return (residual.reshape(rows_local, cols_local, row_width), norms_out)]
    sub x2 -> x0, local copies, waits for them, and re-layouts: 16.4 us -> none  [edge_flux(): return harmonic_mean(low_cond, high_cond) * (high_volt - low_volt)]
    ppermute x4, waiting for transfers between devices: 0.01 us -> 14.5 us  [the longest x2 12 us: neighbours(): low = lax.ppermute(slab(extent - 1), axis, forward)]
  transfers between devices with their start and end apart: 4 -> 4, of which waited for: 0 -> 2; matrix products, arithmetic and copies ran while one was open for 55% -> 1% of each run, Pallas kernels for 0% -> 0%
where the time goes in v1:
time: 139 us
  blocking collectives  82 us (59%)
  Pallas kernels  27.6 us (20%)
  waiting for transfers between devices  14.5 us (10%)
  starting transfers between devices  7.53 us (5%)
  local copies, waits for them, and re-layouts  5.37 us (4%)
    psum x1, blocking collectives, body(): summed = lax.psum(partial, ('gx', 'gy'))  82 us
    pallas_call x1, Pallas kernels, local_residual(): pl.pallas_call(kernel, grid=(PAIRS + 1,), in_specs=[smem, smem, pl.BlockS...  27.6 us
    ppermute x2, waiting for transfers between devices, neighbours(): low = lax.ppermute(slab(extent - 1), axis, forward)  12 us
    ppermute x2, starting transfers between devices, neighbours(): low = lax.ppermute(slab(extent - 1), axis, forward)  6.15 us
  transfers between devices with their start and end apart: 4, of which 2 were waited for; matrix products, arithmetic and copies ran while one was open for 1% of the time, Pallas kernels for 0%

profile of v1, /device:TPU:1, one launch (start us, length us, event | category | flops | bytes accessed | tf_op | source)
XLA Modules:
  0.0 138.7 jit_solution(9265588151913943998)
XLA Ops:
  0.6 0.0 copy-start.6
  0.6 1.3 fusion.4
  2.0 1.1 fusion.5
  3.1 0.1 copy.29
  3.2 4.0 %collective-permute-start.2 = (f32[8,2176]{1,0:T(8,128)S(1)}, f32[8,2176]{1,0:T(8,128)S(1)}, u32[]{:S(2)}, u32[]{:S(2)}) collective-permute-start(f32[8,2176]{1,0:T(8,128)S(1)} %select_maximum_fusion.3), channel_id=1, source_target_pairs={{0,1},{1,2},{2,3},{3,4},{4,5},{5,6},{6,7},{8,9},{9,10},{10,11},{11... | collective-permute-start | bytes 208904 | tf_op jit(solution)/shard_map/ppermute | solution.py:322
  7.3 0.1 copy.31
  7.4 1.3 collective-permute-start.3
  8.7 0.0 copy-done.6
  8.7 0.1 copy.26.region_ref
  8.9 1.3 slice_bitcast_fusion
  10.2 0.0 copy-start.7
  10.2 0.0 copy-start
  10.3 2.1 %collective-permute-start = (f32[64,2176]{1,0:T(8,128)S(1)}, f32[64,2176]{1,0:T(8,128)S(1)}, u32[]{:S(2)}, u32[]{:S(2)}) collective-permute-start(f32[64,2176]{1,0:T(8,128)S(1)} %select_maximum_fusion.1), channel_id=1, source_target_pairs={{0,8},{8,16},{16,24},{24,32},{32,40},{40,48},{48,56},{56,64},{64,7... | collective-permute-start | bytes 1671176 | tf_op jit(solution)/shard_map/ppermute | solution.py:322
  12.4 0.1 collective-permute-start.1
  12.5 0.0 copy-done.7
  12.5 0.1 copy.27.mask_ref
  12.7 0.0 collective-permute-done.2
  12.7 0.0 collective-permute-done.3
  12.8 0.0 copy-done
  12.8 0.1 select_reduce_fusion.col_region
  12.9 12.0 %collective-permute-done = f32[64,2176]{1,0:T(8,128)S(1)} collective-permute-done((f32[64,2176]{1,0:T(8,128)S(1)}, f32[64,2176]{1,0:T(8,128)S(1)}, u32[]{:S(2)}, u32[]{:S(2)}) %collective-permute-start) | collective-permute-done | bytes 557088 | tf_op jit(solution)/shard_map/ppermute | solution.py:322
  24.9 2.6 %collective-permute-done.1 = f32[64,2176]{1,0:T(8,128)S(1)} collective-permute-done((f32[64,2176]{1,0:T(8,128)S(1)}, f32[64,2176]{1,0:T(8,128)S(1)}, u32[]{:S(2)}, u32[]{:S(2)}) %collective-permute-start.1) | collective-permute-done | bytes 557088 | tf_op jit(solution)/shard_map/ppermute | solution.py:323
  27.5 0.0 copy-start.1
  27.5 0.0 copy-start.2
  27.5 0.0 copy-start.3
  27.5 0.0 copy-start.4
  27.5 0.0 copy-start.5
  27.6 0.1 slice.50.row_ref
  27.7 0.5 copy-done.1
  28.1 0.3 copy-done.2
  28.4 0.0 copy-done.3
  28.5 0.0 copy-done.4
  28.5 0.0 copy-done.5
  28.5 27.6 %residual.1 = (f32[8,64,2048]{2,1,0:T(8,128)}, f32[8,128]{1,0:T(8,128)S(1)}) custom-call(f32[8]{0:T(128)S(1)} %copy-done, f32[8]{0:T(128)S(1)} %copy-done.1, f32[8,64,2048]{2,1,0:T(8,128)} %volt_ref.1, f32[8,64,2048]{2,1,0:T(8,128)} %drive_ref.1, s32[8,64,32]{2,1,0:T(8,128)S(1)} %copy.26.region_ref, s32[8,64,32]{2,1,0:T(8,128)S(1)} %copy.27.mask_ref, ...), custom_call_target="tpu_custom_call" | custom-call | flops 4194304000 | bytes 12582912 | tf_op jit(solution)/shard_map/residual/pallas_call | solution.py:253
  56.1 0.1 reduce_sum.27
  56.2 82.0 %psum.7 = f32[64]{0:T(128)S(1)} all-reduce(f32[64]{0:T(128)S(1)} %reduce_sum.28), channel_id=1, replica_groups=mesh['gx'=32,'gy'=8] {'gx','gy'}, use_global_device_ids=true, to_apply=%region_3.4 | all-reduce | flops 64 | bytes 512 | tf_op jit(solution)/shard_map/psum | solution.py:347
  138.2 0.5 add_sqrt_fusion
  (19 shorter events, 0.3 us)
Async XLA Ops:
  0.6 8.1 %copy-start.6 = (s32[8,64,32]{1,2,0:T(8,128)S(1)}, s32[8,64,32]{1,2,0:T(8,128)}, u32[]{:S(2)}) copy-start(s32[8,64,32]{1,2,0:T(8,128)} %param.12) | copy-start | bytes 196612
  3.2 9.5 %collective-permute-start.2 = (f32[8,2176]{1,0:T(8,128)S(1)}, f32[8,2176]{1,0:T(8,128)S(1)}, u32[]{:S(2)}, u32[]{:S(2)}) collective-permute-start(f32[8,2176]{1,0:T(8,128)S(1)} %select_maximum_fusion.3), channel_id=1, source_target_pairs={{0,1},{1,2},{2,3},{3,4},{4,5},{5,6},{6,7},{8,9},{9,10},{10,11},{11... | collective-permute-start | bytes 208904 | tf_op jit(solution)/shard_map/ppermute | solution.py:322
  7.4 5.3 %collective-permute-start.3 = (f32[8,2176]{1,0:T(8,128)S(1)}, f32[8,2176]{1,0:T(8,128)S(1)}, u32[]{:S(2)}, u32[]{:S(2)}) collective-permute-start(f32[8,2176]{1,0:T(8,128)S(1)} %select_maximum_fusion.2), channel_id=1, source_target_pairs={{1,0},{2,1},{3,2},{4,3},{5,4},{6,5},{7,6},{9,8},{10,9},{11,10},{12... | collective-permute-start | bytes 208904 | tf_op jit(solution)/shard_map/ppermute | solution.py:323
  10.2 2.3 %copy-start.7 = (s32[8,64,32]{1,2,0:T(8,128)S(1)}, s32[8,64,32]{1,2,0:T(8,128)}, u32[]{:S(2)}) copy-start(s32[8,64,32]{1,2,0:T(8,128)} %param.13) | copy-start | bytes 196612
  10.2 2.5 %copy-start = (f32[8]{0:T(128)S(1)}, f32[8]{0:T(128)}, u32[]{:S(2)}) copy-start(f32[8]{0:T(128)} %sigma_ref.1) | copy-start | bytes 100
  10.3 14.6 %collective-permute-start = (f32[64,2176]{1,0:T(8,128)S(1)}, f32[64,2176]{1,0:T(8,128)S(1)}, u32[]{:S(2)}, u32[]{:S(2)}) collective-permute-start(f32[64,2176]{1,0:T(8,128)S(1)} %select_maximum_fusion.1), channel_id=1, source_target_pairs={{0,8},{8,16},{16,24},{24,32},{32,40},{40,48},{48,56},{56,64},{64,7... | collective-permute-start | bytes 1671176 | tf_op jit(solution)/shard_map/ppermute | solution.py:322
  12.4 15.0 %collective-permute-start.1 = (f32[64,2176]{1,0:T(8,128)S(1)}, f32[64,2176]{1,0:T(8,128)S(1)}, u32[]{:S(2)}, u32[]{:S(2)}) collective-permute-start(f32[64,2176]{1,0:T(8,128)S(1)} %select_maximum_fusion), channel_id=1, source_target_pairs={{8,0},{16,8},{24,16},{32,24},{40,32},{48,40},{56,48},{64,56},{72,6... | collective-permute-start | bytes 1671176 | tf_op jit(solution)/shard_map/ppermute | solution.py:323
  27.5 0.7 copy-start.1
  27.5 1.0 copy-start.2
  27.5 1.0 copy-start.3
  27.5 1.0 copy-start.4
  27.5 1.0 copy-start.5

commit v2 on v1

v2 whole, which is shorter than its diff:
```python
import functools
import math

import jax
import jax.numpy as jnp
import numpy as np
from jax import lax
from jax.experimental import pallas as pl
from jax.experimental.pallas import tpu as pltpu
from jax.sharding import PartitionSpec as P

NZ = 32
H = 32
KC = 64
S = 256
REGIONS = 8
ROWS = 8
COLS = 64
PAIRS = NZ // 2
LANES = 128
GROUPS = ROWS * COLS // LANES
CELLS = ROWS * COLS
WIDTH = NZ * KC

base_freq = 0.1
norm_eps = 1e-06

GX = 0
GYP = GX + GROUPS + 1
GYM = GYP + GROUPS
GZP = GYM + GROUPS
GZM = GZP + GROUPS
CAP = GZM + GROUPS
DIO = CAP + GROUPS
GSUM = DIO + GROUPS
FIELDS = GSUM + GROUPS

CHUNK = 64


def halves(table):
    high = table.astype(jnp.bfloat16)
    low = (table - high.astype(np.float64)).astype(jnp.bfloat16)
    return high, low


def constant_tables():
    orders = np.arange(1, H + 1, dtype=np.float64)
    angles = orders[:, None] * (2.0 * math.pi * np.arange(S) / S)[None, :]
    cosines, sines = np.cos(angles), np.sin(angles)
    synthesis = np.concatenate([cosines, sines], axis=0)
    high, low = halves(synthesis.T)
    forward = np.concatenate([high, low, high, low], axis=1)
    scaled = base_freq * orders[:, None]
    from_even = halves(synthesis / S)
    from_odd = halves(np.concatenate([scaled * sines, -scaled * cosines], axis=0) / S)
    rows = []
    for part in range(2):
        blocks = []
        for first in range(0, S, CHUNK):
            even = from_even[part][:, first : first + CHUNK]
            odd = from_odd[part][:, first : first + CHUNK]
            blocks += [even, even, odd, odd]
        rows.append(np.concatenate(blocks, axis=1))
    backward = np.concatenate(rows, axis=0).astype(np.float32)
    rates = np.concatenate([scaled, -scaled], axis=0).astype(np.float32)
    rates = np.ascontiguousarray(np.broadcast_to(rates, (KC, LANES)))
    spread = np.zeros((2 * ROWS, CELLS), np.float32)
    for row in range(ROWS):
        group, half = row % GROUPS, row // GROUPS
        spread[row, group * LANES + half * COLS] = 1.0
        spread[ROWS + row, group * LANES + half * COLS + COLS - 1] = 1.0
    widen = np.tile(np.repeat(np.eye(NZ), KC, axis=1), (3, 1)).astype(jnp.bfloat16)
    return forward, backward, rates, spread, widen


def split(values):
    high = values.astype(jnp.bfloat16)
    low = (values - high.astype(jnp.float32)).astype(jnp.bfloat16)
    return high, low


def dot(left, right):
    return jnp.dot(left, right, preferred_element_type=jnp.float32)


def dot_exact(left, right):
    return jnp.dot(
        left, right, preferred_element_type=jnp.float32, precision=lax.Precision.HIGHEST
    )


def harmonic_mean(left, right):
    return 2.0 * left * right / (left + right)


def look_up(region, table_ref):
    found = jnp.zeros(region.shape, jnp.float32)
    for index in range(REGIONS):
        found = jnp.where(region == float(index), table_ref[index], found)
    return found


def in_groups(block, group):
    return jnp.concatenate([block[group], block[group + GROUPS]], axis=0)


def layers_of(ref, pair):
    lanes = pl.ds(pl.multiple_of(pair * LANES, LANES), LANES)
    return ref.at[..., lanes]


def group_lanes(g):
    return slice(g * LANES, (g + 1) * LANES)


def diode_terms(volt, forward, backward):
    high, low = split(volt)
    samples = dot(forward, jnp.concatenate([high, high, low, low], axis=0))
    blocks = []
    for first in range(0, S, CHUNK):
        sample = samples[first : first + CHUNK]
        odd = jnp.tanh(sample)
        even = jnp.abs(sample) - jnp.log(1.0 + jnp.abs(odd))
        coarse = jnp.round(even)
        near = odd.astype(jnp.bfloat16).astype(jnp.float32)
        blocks += [coarse, even - coarse, near, odd - near]
    spectrum = dot(backward, jnp.concatenate(blocks, axis=0))
    return spectrum[:KC] + spectrum[KC:]


def diode_kernel(volt_ref, forward_ref, backward_ref, turned, diode_ref):
    def turn(pair):
        block = layers_of(volt_ref, pair)
        for g in range(GROUPS):
            turned[pair, :, group_lanes(g)] = in_groups(block, g).T

    def at_pair(pair):
        for half in range(2):
            mine = slice(half * KC, (half + 1) * KC)
            diode_ref[pair, mine, :] = diode_terms(
                turned[pair, mine, :], forward_ref[...], backward_ref[...]
            )

    turn(0)

    @pl.loop(0, PAIRS)
    def _(pair):
        at_pair(pair)
        turn(jnp.minimum(pair + 1, PAIRS - 1))


def beside(block, group):
    return jnp.concatenate([block[group], block[group + GROUPS]], axis=1).astype(jnp.float32)


def kinds_of(message):
    return message[:, WIDTH : WIDTH + NZ] - 1.0


def fill_factors(sigma_ref, cap_ref, region_ref, mask_ref, rows, cols, own_cols, spread, factors):
    lane = lax.broadcasted_iota(jnp.int32, (NZ, LANES), 1)
    first = lane < COLS
    column = jnp.where(first, lane, lane - COLS)
    region = [beside(region_ref, g) for g in range(GROUPS)]
    conduct = [look_up(r, sigma_ref) for r in region]
    row_kinds = jnp.concatenate([message[:, WIDTH:] for message in rows], axis=0).T
    row_halo = look_up(row_kinds[:NZ] - 1.0, sigma_ref)
    outer = look_up(jnp.concatenate([kinds_of(m) for m in cols], axis=0), sigma_ref)
    inner = look_up(jnp.concatenate([kinds_of(m) for m in own_cols], axis=0), sigma_ref)
    rim = harmonic_mean(inner, outer)
    rim_spread = dot_exact(rim.T, spread)
    below = jnp.where(first, row_halo, pltpu.roll(conduct[GROUPS - 1], COLS, 1))
    above = jnp.where(first, pltpu.roll(conduct[0], COLS, 1), row_halo)
    stack = [below] + conduct + [above]
    faces = [harmonic_mean(stack[g], stack[g + 1]) for g in range(GROUPS + 1)]
    layer = lax.broadcasted_iota(jnp.int32, (NZ, LANES), 0)
    for g in range(GROUPS + 1):
        factors[GX + g] = faces[g]
    for g in range(GROUPS):
        here = conduct[g]
        plus = harmonic_mean(here, pltpu.roll(here, LANES - 1, 1))
        plus = jnp.where(column == COLS - 1, 0.0, plus)
        minus = jnp.where(column == 0, 0.0, harmonic_mean(here, pltpu.roll(here, 1, 1)))
        upper = harmonic_mean(here, pltpu.roll(here, NZ - 1, 0))
        upper = jnp.where(layer == NZ - 1, 0.0, upper)
        lower = jnp.where(layer == 0, 0.0, harmonic_mean(here, pltpu.roll(here, 1, 0)))
        diode = beside(mask_ref, g)
        factors[GYP + g] = plus
        factors[GYM + g] = minus
        factors[GZP + g] = upper
        factors[GZM + g] = lower
        factors[CAP + g] = look_up(region[g], cap_ref)
        factors[DIO + g] = diode
        factors[GSUM + g] = (
            faces[g] + faces[g + 1] + plus + minus + rim_spread[:, group_lanes(g)]
            + upper + lower + 0.5 * diode
        )
    return rim


def residual_kernel(
    sigma_ref,
    cap_ref,
    turned,
    diode_ref,
    drive_ref,
    region_ref,
    mask_ref,
    row_low,
    row_high,
    col_low,
    col_high,
    own_first,
    own_last,
    rates_ref,
    spread_ref,
    widen_ref,
    out_ref,
    squares_ref,
    factors,
    rim_flux,
    sums,
):
    cols = [col_low[...], col_high[...]]
    rim = fill_factors(
        sigma_ref,
        cap_ref,
        region_ref,
        mask_ref,
        [row_low, row_high],
        cols,
        [own_first[...], own_last[...]],
        spread_ref[...],
        factors,
    )
    top = rim.astype(jnp.bfloat16).astype(jnp.float32)
    middle = (rim - top).astype(jnp.bfloat16).astype(jnp.float32)
    rim = jnp.concatenate([top, middle, rim - top - middle], axis=1).astype(jnp.bfloat16)
    rim_flux[...] = dot(rim, widen_ref[...]) * jnp.concatenate([c[:, :WIDTH] for c in cols], axis=0)
    first = lax.broadcasted_iota(jnp.int32, (KC, LANES), 1) < COLS
    at_low = lax.broadcasted_iota(jnp.int32, (8, LANES), 0) == 0
    at_high = lax.broadcasted_iota(jnp.int32, (8, LANES), 0) == 7

    def gather(pair):
        row_halo = jnp.concatenate(
            [layers_of(row_low, pair)[...], layers_of(row_high, pair)[...]], axis=0
        ).T
        for half in range(2):
            layer = 2 * pair + half
            mine = slice(half * KC, (half + 1) * KC)
            other = slice((1 - half) * KC, (2 - half) * KC)
            before = jnp.maximum(pair - 1, 0) if half == 0 else pair
            after = pair if half == 0 else jnp.minimum(pair + 1, PAIRS - 1)

            def factor(index):
                return factors[index, pl.ds(layer, 1), :]

            volts = [turned[pair, mine, group_lanes(g)] for g in range(GROUPS)]
            halo = row_halo[mine]
            below = jnp.where(first, halo, pltpu.roll(volts[GROUPS - 1], COLS, 1))
            above = jnp.where(first, pltpu.roll(volts[0], COLS, 1), halo)
            stack = [below] + volts + [above]
            for g in range(GROUPS):
                here = volts[g]
                swapped = jnp.concatenate([here[KC // 2 :], here[: KC // 2]], axis=0)
                total = factor(GSUM + g) * here
                total -= factor(GX + g) * stack[g]
                total -= factor(GX + g + 1) * stack[g + 2]
                total -= factor(GYP + g) * pltpu.roll(here, LANES - 1, 1)
                total -= factor(GYM + g) * pltpu.roll(here, 1, 1)
                total -= factor(GZP + g) * turned[after, other, group_lanes(g)]
                total -= factor(GZM + g) * turned[before, other, group_lanes(g)]
                total += factor(CAP + g) * rates_ref[...] * swapped
                total += factor(DIO + g) * diode_ref[pair, mine, group_lanes(g)]
                sums[mine, group_lanes(g)] = total

    def finish(pair, squares):
        drive = layers_of(drive_ref, pair)
        out = layers_of(out_ref, pair)
        edges = layers_of(rim_flux, pair)
        for g in range(GROUPS):
            cells = sums[:, group_lanes(g)].T
            for which in range(2):
                row = g + which * GROUPS
                value = cells[which * COLS : (which + 1) * COLS] - drive[row]
                low = jnp.where(at_low, edges[row : row + 1, :], 0.0)
                high = jnp.where(at_high, edges[ROWS + row : ROWS + row + 1, :], 0.0)
                value = jnp.concatenate(
                    [value[:8] - low, value[8 : COLS - 8], value[COLS - 8 :] - high], axis=0
                )
                out[row] = value
                squares += jnp.sum((value * value).reshape(COLS // 8, 8, LANES), axis=0)
        return squares

    gather(0)

    def step(pair, squares):
        squares = finish(pair - 1, squares)
        gather(pair)
        return squares

    squares = lax.fori_loop(1, PAIRS, step, jnp.zeros((8, LANES), jnp.float32))
    squares = jnp.sum(finish(PAIRS - 1, squares), axis=0, keepdims=True)
    squares += pltpu.roll(squares, KC, 1)
    squares_ref[...] = jnp.broadcast_to(squares, squares_ref.shape)


def in_vmem(count):
    return [pl.BlockSpec(memory_space=pltpu.VMEM)] * count


def pack_kernel(volt_ref, region_ref, row_first, row_last, col_first, col_last):
    kinds = [region_ref[row].astype(jnp.float32).T + 1.0 for row in range(ROWS)]

    def put(message, volts, regions):
        message[:, :WIDTH] = volts
        padding = jnp.zeros((regions.shape[0], LANES - NZ), jnp.float32)
        message[:, WIDTH:] = jnp.concatenate([regions, padding], axis=1)

    put(row_first, volt_ref[0], kinds[0])
    put(row_last, volt_ref[ROWS - 1], kinds[ROWS - 1])
    for message, col in ((col_first, 0), (col_last, COLS - 1)):
        regions = jnp.concatenate([kind[col : col + 1] for kind in kinds], axis=0)
        put(message, volt_ref[:, col, :], regions)


def packed(volt, region):
    shapes = [(COLS, WIDTH + LANES)] * 2 + [(ROWS, WIDTH + LANES)] * 2
    return pl.pallas_call(
        pack_kernel,
        in_specs=in_vmem(2),
        out_specs=in_vmem(4),
        out_shape=[jax.ShapeDtypeStruct(shape, jnp.float32) for shape in shapes],
        compiler_params=pltpu.CompilerParams(vmem_limit_bytes=8 * 1024 * 1024),
        name="pack",
    )(volt, region)


def diode_part(volt):
    forward, backward = constant_tables()[:2]
    samples = CELLS * NZ * S
    whole = jax.ShapeDtypeStruct((PAIRS, LANES, CELLS), jnp.float32)
    return pl.pallas_call(
        diode_kernel,
        in_specs=in_vmem(3),
        out_specs=in_vmem(2),
        out_shape=[whole, whole],
        compiler_params=pltpu.CompilerParams(vmem_limit_bytes=16 * 1024 * 1024),
        cost_estimate=pl.CostEstimate(
            flops=samples * 1000, bytes_accessed=4 * CELLS * WIDTH, transcendentals=2 * samples
        ),
        name="diode",
    )(volt, jnp.asarray(forward), jnp.asarray(backward))


def whole_residual(turned, diode, drive, region, mask, halos, own_cols, tables, copies):
    rates, spread, widen = constant_tables()[2:]
    smem = pl.BlockSpec(memory_space=pltpu.SMEM)
    return pl.pallas_call(
        residual_kernel,
        in_specs=[smem, smem] + in_vmem(14),
        out_specs=in_vmem(2),
        out_shape=[
            jax.ShapeDtypeStruct((ROWS, COLS, WIDTH), jnp.float32),
            jax.ShapeDtypeStruct((copies, LANES), jnp.float32),
        ],
        scratch_shapes=[
            pltpu.VMEM((FIELDS, NZ, LANES), jnp.float32),
            pltpu.VMEM((2 * ROWS, WIDTH), jnp.float32),
            pltpu.VMEM((LANES, CELLS), jnp.float32),
        ],
        compiler_params=pltpu.CompilerParams(vmem_limit_bytes=16 * 1024 * 1024),
        cost_estimate=pl.CostEstimate(
            flops=30 * CELLS * WIDTH, bytes_accessed=2 * 4 * CELLS * WIDTH, transcendentals=0
        ),
        name="residual",
    )(
        *tables,
        turned,
        diode,
        drive,
        region,
        mask,
        *halos,
        *own_cols,
        jnp.asarray(rates),
        jnp.asarray(spread),
        jnp.asarray(widen),
    )


def neighbours(first, last, axis, periodic):
    count = lax.axis_size(axis)
    forward = [(i, i + 1) for i in range(count - 1)]
    if periodic:
        forward.append((count - 1, 0))
    backward = [(target, source) for source, target in forward]
    return lax.ppermute(last, axis, forward), lax.ppermute(first, axis, backward)


def exchanged_sum(copies, axis):
    return jnp.sum(lax.all_to_all(copies, axis, 0, 0, tiled=True), axis=0)


def body(volt, drive, region, diode_mask, sigma_table, cap_table):
    by_layer = jnp.transpose(region, (0, 2, 1))
    mask = jnp.transpose(diode_mask, (0, 2, 1))
    row_first, row_last, col_first, col_last = packed(volt, by_layer)
    rows = neighbours(row_first, row_last, "gx", True)
    cols = neighbours(col_first, col_last, "gy", False)
    turned, diode = diode_part(volt)
    nx, ny = lax.axis_size("gx"), lax.axis_size("gy")
    residual, squares = whole_residual(
        turned,
        diode,
        drive,
        by_layer,
        mask,
        rows + cols,
        (col_first, col_last),
        (sigma_table, cap_table),
        nx,
    )
    over_x = exchanged_sum(squares, "gx")
    summed = exchanged_sum(jnp.broadcast_to(over_x, (ny, LANES)), "gy")[:KC]
    return residual, jnp.sqrt(summed / (CELLS * NZ * nx * ny) + norm_eps)


def solution(mesh):
    spec = P("gx", "gy", None)
    return jax.shard_map(
        body,
        mesh=mesh,
        in_specs=(spec, spec, spec, spec, P(), P()),
        out_specs=(spec, P()),
        check_vma=False,
    )
```

time: 139 us -> 75 us (0.54)
  blocking collectives: 82 us -> 34.4 us
  waiting for transfers between devices: 14.5 us -> 0.01 us
    psum x1 -> x0, blocking collectives: 82 us -> none  [body(): summed = lax.psum(partial, ('gx', 'gy'))]
    all_to_all x0 -> x2, blocking collectives: none -> 34.4 us  [exchanged_sum(): return jnp.sum(lax.all_to_all(copies, axis, 0, 0, tiled=True), axis=0)]
    ppermute x4, waiting for transfers between devices: 14.5 us -> 0.01 us  [the longest x2 0.01 us: neighbours(): lax.ppermute(first, axis, backward)]
    unnamed x24 -> x26, local copies, waits for them, and re-layouts: 1.44 us -> 4.18 us
    slice x5 -> x0, local copies, waits for them, and re-layouts: 2.51 us -> none  [the longest x1 1.33 us: slab(): cells = lax.index_in_dim(volt, index, dim, keepdims=False)]
    pallas_call x1 -> x3, Pallas kernels: 27.6 us -> 27.2 us  [the longest x1 17.6 us: diode_part(): pl.pallas_call(diode_kernel, in_specs=in_vmem(3), out_specs=in_vmem(2), o...]
  transfers between devices with their start and end apart: 4 -> 4, of which waited for: 2 -> 0; matrix products, arithmetic and copies ran while one was open for 1% -> 0% of each run, Pallas kernels for 0% -> 24%
where the time goes in v2:
time: 75 us; the launch traced here: 74.7 us
  blocking collectives  34.4 us (46%)
  Pallas kernels  27.2 us (36%)
  starting transfers between devices  7.42 us (10%)
  local copies, waits for them, and re-layouts  4.19 us (6%)
  between operations  0.86 us (1%)
    all_to_all x2, blocking collectives, exchanged_sum(): return jnp.sum(lax.all_to_all(copies, axis, 0, 0, tiled=True), axis=0)  34.4 us
    pallas_call x1, Pallas kernels, diode_part(): pl.pallas_call(diode_kernel, in_specs=in_vmem(3), out_specs=in_vmem(2), o...  17.6 us
    pallas_call x1, Pallas kernels, whole_residual(): pl.pallas_call(residual_kernel, in_specs=[smem, smem] + in_vmem(14), out_...  9.54 us
    ppermute x2, starting transfers between devices, neighbours(): lax.ppermute(last, axis, forward)  5.16 us
    unnamed x26, local copies, waits for them, and re-layouts  4.18 us
    ppermute x2, starting transfers between devices, neighbours(): lax.ppermute(first, axis, backward)  2.26 us
  transfers between devices with their start and end apart: 4, of which 0 were waited for; matrix products, arithmetic and copies ran while one was open for 0% of the time, Pallas kernels for 24%

profile of v2, /device:TPU:1, one launch (start us, length us, event | category | flops | bytes accessed | tf_op | source)
XLA Modules:
  0.0 74.7 jit_solution(1371670728335803522)
XLA Ops:
  0.6 0.0 copy-start.1
  0.6 2.2 %copy-done.1 = f32[8,64,2048]{2,1,0:T(8,128)S(1)} copy-done((f32[8,64,2048]{2,1,0:T(8,128)S(1)}, f32[8,64,2048]{2,1,0:T(8,128)}, u32[]{:S(2)}) %copy-start.1) | copy-done | bytes 4194328
  2.8 0.0 copy-start.3
  2.8 0.9 %copy-done.3 = s32[8,64,32]{1,2,0:T(8,128)S(1)} copy-done((s32[8,64,32]{1,2,0:T(8,128)S(1)}, s32[8,64,32]{1,2,0:T(8,128)}, u32[]{:S(2)}) %copy-start.3) | copy-done | bytes 65560
  3.7 0.0 copy-start.2
  3.7 0.0 copy-start.12
  3.7 0.1 pack.1
  3.9 2.7 %collective-permute-start = (f32[64,2176]{1,0:T(8,128)S(1)}, f32[64,2176]{1,0:T(8,128)S(1)}, u32[]{:S(2)}, u32[]{:S(2)}) collective-permute-start(f32[64,2176]{1,0:T(8,128)S(1)} %get-tuple-element.12), channel_id=1, source_target_pairs={{0,8},{8,16},{16,24},{24,32},{32,40},{40,48},{48,56},{56,64},{64,7... | collective-permute-start | bytes 1671176 | tf_op jit(solution)/shard_map/ppermute | solution.py:399
  6.5 0.7 collective-permute-start.1
  7.2 2.5 %collective-permute-start.2 = (f32[8,2176]{1,0:T(8,128)S(1)}, f32[8,2176]{1,0:T(8,128)S(1)}, u32[]{:S(2)}, u32[]{:S(2)}) collective-permute-start(f32[8,2176]{1,0:T(8,128)S(1)} %get-tuple-element.14.own_last), channel_id=1, source_target_pairs={{0,1},{1,2},{2,3},{3,4},{4,5},{5,6},{6,7},{8,9},{9,10},{10,11},{11... | collective-permute-start | bytes 208904 | tf_op jit(solution)/shard_map/ppermute | solution.py:399
  9.7 0.0 copy-start
  9.8 0.0 copy-start.4
  9.8 0.0 copy-start.5
  9.8 0.0 copy-start.6
  9.8 0.0 copy-start.7
  9.8 0.0 copy-start.8
  9.8 0.0 copy-start.9
  9.8 0.0 copy-start.10
  9.8 1.6 %collective-permute-start.3 = (f32[8,2176]{1,0:T(8,128)S(1)}, f32[8,2176]{1,0:T(8,128)S(1)}, u32[]{:S(2)}, u32[]{:S(2)}) collective-permute-start(f32[8,2176]{1,0:T(8,128)S(1)} %get-tuple-element.15.own_first), channel_id=1, source_target_pairs={{1,0},{2,1},{3,2},{4,3},{5,4},{6,5},{7,6},{9,8},{10,9},{11,10},{12... | collective-permute-start | bytes 208904 | tf_op jit(solution)/shard_map/ppermute | solution.py:399
  11.4 0.0 copy-done.2
  11.4 0.0 copy-done.12
  11.4 0.0 copy-start.11
  11.4 1.0 %copy-done.11 = f32[128,1024]{1,0:T(8,128)S(1)} copy-done((f32[128,1024]{1,0:T(8,128)S(1)}, f32[128,1024]{1,0:T(8,128)}, u32[]{:S(2)}) %copy-start.11) | copy-done | bytes 524312
  12.5 17.6 %diode.1 = (f32[16,128,512]{2,1,0:T(8,128)S(1)}, f32[16,128,512]{2,1,0:T(8,128)S(1)}) custom-call(f32[8,64,2048]{2,1,0:T(8,128)S(1)} %copy-done.2, bf16[256,256]{1,0:T(8,128)(2,1)S(1)} %copy-done.12, f32[128,1024]{1,0:T(8,128)S(1)} %copy-done.11), custom_call_target="tpu_custom_call" | custom-call | flops 4194304000 | bytes 4194304 | tf_op jit(solution)/shard_map/diode/pallas_call | solution.py:344
  30.0 0.0 collective-permute-done.2.col_low
  30.0 0.0 collective-permute-done.3.col_high
  30.1 0.0 collective-permute-done.row_low
  30.1 0.0 collective-permute-done.1.row_high
  30.1 0.0 copy-done
  30.1 0.0 copy-done.4
  30.1 0.0 copy-done.5
  30.1 0.0 copy-done.6
  30.1 0.0 copy-done.7
  30.1 0.0 copy-done.8
  30.1 0.0 copy-done.9
  30.1 0.0 copy-done.10
  30.2 9.5 %residual.1 = (f32[8,64,2048]{2,1,0:T(8,128)}, f32[32,128]{1,0:T(8,128)S(1)}) custom-call(f32[8]{0:T(128)S(1)} %copy-done.9, f32[8]{0:T(128)S(1)} %copy-done.10, f32[16,128,512]{2,1,0:T(8,128)S(1)} %get-tuple-element.10.turned, f32[16,128,512]{2,1,0:T(8,128)S(1)} %get-tuple-element.11.diode_ref, f32[8,64,2048]{2,1,0:T(8,128)S(1)} %copy-done, ...), custom_call_target="tpu_custom_call" | custom-call | flops 31457280 | bytes 8388608 | tf_op jit(solution)/shard_map/residual/pallas_call | solution.py:360
  39.7 19.3 %all_to_all.15 = f32[32,1,128]{2,1,0:T(1,128)S(1)} all-to-all(f32[32,1,128]{2,1,0:T(1,128)S(1)} %bitcast.9), channel_id=1, replica_groups=mesh['gx'=32,'gy'=8] {'gx'}, dimensions={0} | all-to-all | bytes 32768 | tf_op jit(solution)/shard_map/all_to_all | solution.py:403
  59.0 0.1 reduce_sum.18
  59.1 15.0 %all_to_all.16 = f32[8,1,128]{2,1,0:T(1,128)S(1)} all-to-all(f32[8,1,128]{2,1,0:T(1,128)S(1)} %broadcast_in_dim.3), channel_id=1, replica_groups=mesh['gx'=32,'gy'=8] {'gy'}, dimensions={0} | all-to-all | bytes 8192 | tf_op jit(solution)/shard_map/all_to_all | solution.py:403
  74.1 0.5 add_sqrt_fusion
  (2 shorter events, 0.0 us)
Async XLA Ops:
  0.6 2.2 %copy-start.1 = (f32[8,64,2048]{2,1,0:T(8,128)S(1)}, f32[8,64,2048]{2,1,0:T(8,128)}, u32[]{:S(2)}) copy-start(f32[8,64,2048]{2,1,0:T(8,128)} %volt_ref.3) | copy-start | bytes 12582916
  2.8 0.9 %copy-start.3 = (s32[8,64,32]{1,2,0:T(8,128)S(1)}, s32[8,64,32]{1,2,0:T(8,128)}, u32[]{:S(2)}) copy-start(s32[8,64,32]{1,2,0:T(8,128)} %param.13) | copy-start | bytes 196612
  3.7 7.7 %copy-start.2 = (f32[8,64,2048]{2,1,0:T(8,128)S(1)}, f32[8,64,2048]{2,1,0:T(8,128)}, u32[]{:S(2)}) copy-start(f32[8,64,2048]{2,1,0:T(8,128)} %volt_ref.3) | copy-start | bytes 12582916
  3.7 7.7 %copy-start.12 = (bf16[256,256]{1,0:T(8,128)(2,1)S(1)}, bf16[256,256]{1,0:T(8,128)(2,1)}, u32[]{:S(2)}) copy-start(bf16[256,256]{1,0:T(8,128)(2,1)} %constant.17.clone.forward_ref) | copy-start | bytes 393220
  3.9 26.2 %collective-permute-start = (f32[64,2176]{1,0:T(8,128)S(1)}, f32[64,2176]{1,0:T(8,128)S(1)}, u32[]{:S(2)}, u32[]{:S(2)}) collective-permute-start(f32[64,2176]{1,0:T(8,128)S(1)} %get-tuple-element.12), channel_id=1, source_target_pairs={{0,8},{8,16},{16,24},{24,32},{32,40},{40,48},{48,56},{56,64},{64,7... | collective-permute-start | bytes 1671176 | tf_op jit(solution)/shard_map/ppermute | solution.py:399
  6.5 23.5 %collective-permute-start.1 = (f32[64,2176]{1,0:T(8,128)S(1)}, f32[64,2176]{1,0:T(8,128)S(1)}, u32[]{:S(2)}, u32[]{:S(2)}) collective-permute-start(f32[64,2176]{1,0:T(8,128)S(1)} %get-tuple-element.13), channel_id=1, source_target_pairs={{8,0},{16,8},{24,16},{32,24},{40,32},{48,40},{56,48},{64,56},{72,6... | collective-permute-start | bytes 1671176 | tf_op jit(solution)/shard_map/ppermute | solution.py:399
  7.2 22.8 %collective-permute-start.2 = (f32[8,2176]{1,0:T(8,128)S(1)}, f32[8,2176]{1,0:T(8,128)S(1)}, u32[]{:S(2)}, u32[]{:S(2)}) collective-permute-start(f32[8,2176]{1,0:T(8,128)S(1)} %get-tuple-element.14.own_last), channel_id=1, source_target_pairs={{0,1},{1,2},{2,3},{3,4},{4,5},{5,6},{6,7},{8,9},{9,10},{10,11},{11... | collective-permute-start | bytes 208904 | tf_op jit(solution)/shard_map/ppermute | solution.py:399
  9.7 20.3 %copy-start = (f32[8,64,2048]{2,1,0:T(8,128)S(1)}, f32[8,64,2048]{2,1,0:T(8,128)}, u32[]{:S(2)}) copy-start(f32[8,64,2048]{2,1,0:T(8,128)} %drive_ref.1) | copy-start | bytes 12582916
  9.8 20.3 %copy-start.4 = (s32[8,64,32]{1,2,0:T(8,128)S(1)}, s32[8,64,32]{1,2,0:T(8,128)}, u32[]{:S(2)}) copy-start(s32[8,64,32]{1,2,0:T(8,128)} %param.13) | copy-start | bytes 196612
  9.8 20.3 %copy-start.5 = (bf16[96,2048]{1,0:T(8,128)(2,1)S(1)}, bf16[96,2048]{1,0:T(8,128)(2,1)}, u32[]{:S(2)}) copy-start(bf16[96,2048]{1,0:T(8,128)(2,1)} %constant.21.clone.widen_ref) | copy-start | bytes 1179652
  9.8 20.3 %copy-start.6 = (s32[8,64,32]{1,2,0:T(8,128)S(1)}, s32[8,64,32]{1,2,0:T(8,128)}, u32[]{:S(2)}) copy-start(s32[8,64,32]{1,2,0:T(8,128)} %param.14) | copy-start | bytes 196612
  9.8 20.3 %copy-start.7 = (f32[16,512]{1,0:T(8,128)S(1)}, f32[16,512]{1,0:T(8,128)}, u32[]{:S(2)}) copy-start(f32[16,512]{1,0:T(8,128)} %constant.20.clone.spread_ref) | copy-start | bytes 98308
  9.8 20.3 %copy-start.8 = (f32[64,128]{1,0:T(8,128)S(1)}, f32[64,128]{1,0:T(8,128)}, u32[]{:S(2)}) copy-start(f32[64,128]{1,0:T(8,128)} %constant.19.clone.rates_ref) | copy-start | bytes 98308
  9.8 20.3 %copy-start.9 = (f32[8]{0:T(128)S(1)}, f32[8]{0:T(128)}, u32[]{:S(2)}) copy-start(f32[8]{0:T(128)} %sigma_ref.1) | copy-start | bytes 100
  9.8 20.3 %copy-start.10 = (f32[8]{0:T(128)S(1)}, f32[8]{0:T(128)}, u32[]{:S(2)}) copy-start(f32[8]{0:T(128)} %cap_ref.1) | copy-start | bytes 100
  9.8 20.2 %collective-permute-start.3 = (f32[8,2176]{1,0:T(8,128)S(1)}, f32[8,2176]{1,0:T(8,128)S(1)}, u32[]{:S(2)}, u32[]{:S(2)}) collective-permute-start(f32[8,2176]{1,0:T(8,128)S(1)} %get-tuple-element.15.own_first), channel_id=1, source_target_pairs={{1,0},{2,1},{3,2},{4,3},{5,4},{6,5},{7,6},{9,8},{10,9},{11,10},{12... | collective-permute-start | bytes 208904 | tf_op jit(solution)/shard_map/ppermute | solution.py:399
  11.4 1.0 %copy-start.11 = (f32[128,1024]{1,0:T(8,128)S(1)}, f32[128,1024]{1,0:T(8,128)}, u32[]{:S(2)}) copy-start(f32[128,1024]{1,0:T(8,128)} %constant.18.clone.backward_ref) | copy-start | bytes 1572868

commit v3 on v2

--- a/solution.py
+++ b/solution.py
@@ -34,6 +34,9 @@
 DIO = CAP + GROUPS
 GSUM = DIO + GROUPS
 FIELDS = GSUM + GROUPS
+
+UNROLL = 2
+PACK_MIB = 46
 
 CHUNK = 64
 
@@ -114,40 +117,60 @@
     return slice(g * LANES, (g + 1) * LANES)
 
 
-def diode_terms(volt, forward, backward):
+def sampled(volt, forward):
     high, low = split(volt)
-    samples = dot(forward, jnp.concatenate([high, high, low, low], axis=0))
-    blocks = []
+    return dot(forward, jnp.concatenate([high, high, low, low], axis=0))
+
+
+def bend(samples, bent):
     for first in range(0, S, CHUNK):
         sample = samples[first : first + CHUNK]
         odd = jnp.tanh(sample)
         even = jnp.abs(sample) - jnp.log(1.0 + jnp.abs(odd))
         coarse = jnp.round(even)
         near = odd.astype(jnp.bfloat16).astype(jnp.float32)
-        blocks += [coarse, even - coarse, near, odd - near]
-    spectrum = dot(backward, jnp.concatenate(blocks, axis=0))
-    return spectrum[:KC] + spectrum[KC:]
-
-
-def diode_kernel(volt_ref, forward_ref, backward_ref, turned, diode_ref):
+        for index, term in enumerate((coarse, even - coarse, near, odd - near)):
+            row = 4 * first + index * CHUNK
+            bent[row : row + CHUNK] = term
+
+
+def diode_kernel(volt_ref, forward_ref, backward_ref, turned, diode_ref, *scratch):
+    samples, bents = scratch[:2], scratch[2:]
+
     def turn(pair):
         block = layers_of(volt_ref, pair)
         for g in range(GROUPS):
             turned[pair, :, group_lanes(g)] = in_groups(block, g).T
 
+    def sample(pair, half):
+        mine = slice(half * KC, (half + 1) * KC)
+        samples[half][...] = sampled(turned[pair, mine, :], forward_ref[...])
+
+    def project(pair, half):
+        mine = slice(half * KC, (half + 1) * KC)
+        spectrum = dot(backward_ref[...], bents[half][...])
+        diode_ref[pair, mine, :] = spectrum[:KC] + spectrum[KC:]
+
+    turn(0)
+    turn(1)
+    sample(0, 0)
+    bents[1][...] = jnp.zeros(bents[1].shape, jnp.float32)
+
     def at_pair(pair):
-        for half in range(2):
-            mine = slice(half * KC, (half + 1) * KC)
-            diode_ref[pair, mine, :] = diode_terms(
-                turned[pair, mine, :], forward_ref[...], backward_ref[...]
-            )
-
-    turn(0)
-
-    @pl.loop(0, PAIRS)
-    def _(pair):
-        at_pair(pair)
-        turn(jnp.minimum(pair + 1, PAIRS - 1))
+        sample(pair, 1)
+        project(jnp.maximum(pair - 1, 0), 1)
+        bend(samples[0], bents[0])
+        sample(jnp.minimum(pair + 1, PAIRS - 1), 0)
+        bend(samples[1], bents[1])
+        project(pair, 0)
+        turn(jnp.minimum(pair + 2, PAIRS - 1))
+
+    @pl.loop(0, PAIRS // UNROLL)
+    def _(block):
+        for index in range(UNROLL):
+            at_pair(UNROLL * block + index)
+
+    project(PAIRS - 1, 1)
 
 
 def beside(block, group):
@@ -220,8 +243,9 @@
     squares_ref,
     factors,
     rim_flux,
-    sums,
+    *scratch,
 ):
+    sums, ready, sent = scratch[:2], scratch[2], scratch[3]
     cols = [col_low[...], col_high[...]]
     rim = fill_factors(
         sigma_ref,
@@ -242,7 +266,7 @@
     at_low = lax.broadcasted_iota(jnp.int32, (8, LANES), 0) == 0
     at_high = lax.broadcasted_iota(jnp.int32, (8, LANES), 0) == 7
 
-    def gather(pair):
+    def gather(pair, slot):
         row_halo = jnp.concatenate(
             [layers_of(row_low, pair)[...], layers_of(row_high, pair)[...]], axis=0
         ).T
@@ -273,14 +297,16 @@
                 total -= factor(GZM + g) * turned[before, other, group_lanes(g)]
                 total += factor(CAP + g) * rates_ref[...] * swapped
                 total += factor(DIO + g) * diode_ref[pair, mine, group_lanes(g)]
-                sums[mine, group_lanes(g)] = total
-
-    def finish(pair, squares):
+                sums[slot][mine, group_lanes(g)] = total
+
+    def copy_out(pair):
+        return pltpu.make_async_copy(ready.at[pair], layers_of(out_ref, pair), sent.at[pair])
+
+    def finish(pair, slot, squares):
         drive = layers_of(drive_ref, pair)
-        out = layers_of(out_ref, pair)
         edges = layers_of(rim_flux, pair)
         for g in range(GROUPS):
-            cells = sums[:, group_lanes(g)].T
+            cells = sums[slot][:, group_lanes(g)].T
             for which in range(2):
                 row = g + which * GROUPS
                 value = cells[which * COLS : (which + 1) * COLS] - drive[row]
@@ -289,28 +315,47 @@
                 value = jnp.concatenate(
                     [value[:8] - low, value[8 : COLS - 8], value[COLS - 8 :] - high], axis=0
                 )
-                out[row] = value
+                ready[pair, row] = value
                 squares += jnp.sum((value * value).reshape(COLS // 8, 8, LANES), axis=0)
         return squares
 
-    gather(0)
-
-    def step(pair, squares):
-        squares = finish(pair - 1, squares)
-        gather(pair)
+    for slot in range(2):
+        gather(slot, slot)
+
+    def step(index, squares):
+        pair = 2 * index
+        for slot in range(2):
+            squares = finish(pair - 2 + slot, slot, squares)
+            gather(pair + slot, slot)
+        for slot in range(2):
+            copy_out(pair - 2 + slot).start()
         return squares
 
-    squares = lax.fori_loop(1, PAIRS, step, jnp.zeros((8, LANES), jnp.float32))
-    squares = jnp.sum(finish(PAIRS - 1, squares), axis=0, keepdims=True)
+    squares = lax.fori_loop(1, PAIRS // 2, step, jnp.zeros((8, LANES), jnp.float32))
+    for slot in range(2):
+        squares = finish(PAIRS - 2 + slot, slot, squares)
+        copy_out(PAIRS - 2 + slot).start()
+    squares = jnp.sum(squares, axis=0, keepdims=True)
     squares += pltpu.roll(squares, KC, 1)
     squares_ref[...] = jnp.broadcast_to(squares, squares_ref.shape)
+    for pair in range(PAIRS):
+        copy_out(pair).wait()
 
 
 def in_vmem(count):
     return [pl.BlockSpec(memory_space=pltpu.VMEM)] * count
 
 
-def pack_kernel(volt_ref, region_ref, row_first, row_last, col_first, col_last):
+def pack_kernel(volt_hbm, region_hbm, *refs):
+    row_first, row_last, col_first, col_last, volt_ref, region_ref, arrived = refs
+    fetches = [
+        pltpu.make_async_copy(volt_hbm.at[row], volt_ref.at[row], arrived.at[row])
+        for row in range(ROWS)
+    ]
+    fetches.append(pltpu.make_async_copy(region_hbm, region_ref, arrived.at[ROWS]))
+    for fetch in reversed(fetches):
+        fetch.start()
+    fetches[ROWS].wait()
     kinds = [region_ref[row].astype(jnp.float32).T + 1.0 for row in range(ROWS)]
 
     def put(message, volts, regions):
@@ -318,21 +363,27 @@
         padding = jnp.zeros((regions.shape[0], LANES - NZ), jnp.float32)
         message[:, WIDTH:] = jnp.concatenate([regions, padding], axis=1)
 
+    for row in reversed(range(ROWS)):
+        fetches[row].wait()
+    put(row_last, volt_ref[ROWS - 1], kinds[ROWS - 1])
     put(row_first, volt_ref[0], kinds[0])
-    put(row_last, volt_ref[ROWS - 1], kinds[ROWS - 1])
     for message, col in ((col_first, 0), (col_last, COLS - 1)):
         regions = jnp.concatenate([kind[col : col + 1] for kind in kinds], axis=0)
         put(message, volt_ref[:, col, :], regions)
 
 
 def packed(volt, region):
-    shapes = [(COLS, WIDTH + LANES)] * 2 + [(ROWS, WIDTH + LANES)] * 2
+    shapes = [(COLS, WIDTH + LANES)] * 2 + [(ROWS, WIDTH + LANES)] * 2 + [volt.shape]
     return pl.pallas_call(
         pack_kernel,
-        in_specs=in_vmem(2),
-        out_specs=in_vmem(4),
+        in_specs=[pl.BlockSpec(memory_space=pltpu.HBM)] * 2,
+        out_specs=in_vmem(5),
         out_shape=[jax.ShapeDtypeStruct(shape, jnp.float32) for shape in shapes],
-        compiler_params=pltpu.CompilerParams(vmem_limit_bytes=8 * 1024 * 1024),
+        scratch_shapes=[
+            pltpu.VMEM(region.shape, region.dtype),
+            pltpu.SemaphoreType.DMA((ROWS + 1,)),
+        ],
+        compiler_params=pltpu.CompilerParams(vmem_limit_bytes=PACK_MIB * 1024 * 1024),
         name="pack",
     )(volt, region)
 
@@ -346,6 +397,8 @@
         in_specs=in_vmem(3),
         out_specs=in_vmem(2),
         out_shape=[whole, whole],
+        scratch_shapes=[pltpu.VMEM((S, CELLS), jnp.float32)] * 2
+        + [pltpu.VMEM((4 * S, CELLS), jnp.float32)] * 2,
         compiler_params=pltpu.CompilerParams(vmem_limit_bytes=16 * 1024 * 1024),
         cost_estimate=pl.CostEstimate(
             flops=samples * 1000, bytes_accessed=4 * CELLS * WIDTH, transcendentals=2 * samples
@@ -360,7 +413,7 @@
     return pl.pallas_call(
         residual_kernel,
         in_specs=[smem, smem] + in_vmem(14),
-        out_specs=in_vmem(2),
+        out_specs=[pl.BlockSpec(memory_space=pltpu.HBM)] + in_vmem(1),
         out_shape=[
             jax.ShapeDtypeStruct((ROWS, COLS, WIDTH), jnp.float32),
             jax.ShapeDtypeStruct((copies, LANES), jnp.float32),
@@ -369,6 +422,9 @@
             pltpu.VMEM((FIELDS, NZ, LANES), jnp.float32),
             pltpu.VMEM((2 * ROWS, WIDTH), jnp.float32),
             pltpu.VMEM((LANES, CELLS), jnp.float32),
+            pltpu.VMEM((LANES, CELLS), jnp.float32),
+            pltpu.VMEM((PAIRS, ROWS, COLS, LANES), jnp.float32),
+            pltpu.SemaphoreType.DMA((PAIRS,)),
         ],
         compiler_params=pltpu.CompilerParams(vmem_limit_bytes=16 * 1024 * 1024),
         cost_estimate=pl.CostEstimate(
@@ -406,7 +462,7 @@
 def body(volt, drive, region, diode_mask, sigma_table, cap_table):
     by_layer = jnp.transpose(region, (0, 2, 1))
     mask = jnp.transpose(diode_mask, (0, 2, 1))
-    row_first, row_last, col_first, col_last = packed(volt, by_layer)
+    row_first, row_last, col_first, col_last, volt = packed(volt, by_layer)
     rows = neighbours(row_first, row_last, "gx", True)
     cols = neighbours(col_first, col_last, "gy", False)
     turned, diode = diode_part(volt)

time: 75 us -> 68.6 us (0.915)
  local copies, waits for them, and re-layouts: 4.19 us -> 0.96 us
  Pallas kernels: 27.2 us -> 24.4 us
    pallas_call x1, Pallas kernels: 17.6 us -> 14.3 us  [diode_part(): pl.pallas_call(diode_kernel, in_specs=in_vmem(3), out_specs=in_vmem(2), o...]
    unnamed x26 -> x20, local copies, waits for them, and re-layouts: 4.18 us -> 0.95 us
    pallas_call x1, Pallas kernels: 0.14 us -> 2.52 us  [packed(): pl.pallas_call(pack_kernel, in_specs=[pl.BlockSpec(memory_space=pltpu.HBM...]
    pallas_call x1, Pallas kernels: 9.54 us -> 7.61 us  [whole_residual(): pl.pallas_call(residual_kernel, in_specs=[smem, smem] + in_vmem(14), out_...]
  transfers between devices with their start and end apart: 4 -> 4, of which waited for: 0 -> 0; matrix products, arithmetic and copies ran while one was open for 0% -> 0% of each run, Pallas kernels for 24% -> 21%
where the time goes in v3:
time: 68.6 us; the launch traced here: 68.3 us
  blocking collectives  34.4 us (50%)
  Pallas kernels  24.4 us (36%)
  starting transfers between devices  7.15 us (10%)
  local copies, waits for them, and re-layouts  0.96 us (1%)
  between operations  0.84 us (1%)
    all_to_all x2, blocking collectives, exchanged_sum(): return jnp.sum(lax.all_to_all(copies, axis, 0, 0, tiled=True), axis=0)  34.4 us
    pallas_call x1, Pallas kernels, diode_part(): pl.pallas_call(diode_kernel, in_specs=in_vmem(3), out_specs=in_vmem(2), o...  14.3 us
    pallas_call x1, Pallas kernels, whole_residual(): pl.pallas_call(residual_kernel, in_specs=[smem, smem] + in_vmem(14), out_...  7.61 us
    ppermute x2, starting transfers between devices, neighbours(): lax.ppermute(last, axis, forward)  5.16 us
    pallas_call x1, Pallas kernels, packed(): pl.pallas_call(pack_kernel, in_specs=[pl.BlockSpec(memory_space=pltpu.HBM...  2.52 us
    ppermute x2, starting transfers between devices, neighbours(): lax.ppermute(first, axis, backward)  1.99 us
  transfers between devices with their start and end apart: 4, of which 0 were waited for; matrix products, arithmetic and copies ran while one was open for 0% of the time, Pallas kernels for 21%

profile of v3, /device:TPU:1, one launch (start us, length us, event | category | flops | bytes accessed | tf_op | source)
XLA Modules:
  0.0 68.3 jit_solution(11766111955751487062)
XLA Ops:
  0.6 0.0 copy-start.1
  0.6 0.9 %copy-done.1 = s32[8,64,32]{1,2,0:T(8,128)S(1)} copy-done((s32[8,64,32]{1,2,0:T(8,128)S(1)}, s32[8,64,32]{1,2,0:T(8,128)}, u32[]{:S(2)}) %copy-start.1) | copy-done | bytes 65560
  1.5 0.0 copy-start.8
  1.5 0.0 copy-start.9
  1.5 2.5 %pack.1 = (f32[64,2176]{1,0:T(8,128)S(1)}, f32[64,2176]{1,0:T(8,128)S(1)}, f32[8,2176]{1,0:T(8,128)S(1)}, f32[8,2176]{1,0:T(8,128)S(1)}, f32[8,64,2048]{2,1,0:T(8,128)S(1)}) custom-call(f32[8,64,2048]{2,1,0:T(8,128)} %volt_hbm.1, s32[8,32,64]{2,1,0:T(8,128)S(1)} %bitcast.6), custom_call_target="tpu_custom_call" | custom-call | tf_op jit(solution)/shard_map/pack/pallas_call | solution.py:377
  4.1 2.7 %collective-permute-start = (f32[64,2176]{1,0:T(8,128)S(1)}, f32[64,2176]{1,0:T(8,128)S(1)}, u32[]{:S(2)}, u32[]{:S(2)}) collective-permute-start(f32[64,2176]{1,0:T(8,128)S(1)} %get-tuple-element.14), channel_id=1, source_target_pairs={{0,8},{8,16},{16,24},{24,32},{32,40},{40,48},{48,56},{56,64},{64,7... | collective-permute-start | bytes 1671176 | tf_op jit(solution)/shard_map/ppermute | solution.py:455
  6.7 0.7 %collective-permute-start.1 = (f32[64,2176]{1,0:T(8,128)S(1)}, f32[64,2176]{1,0:T(8,128)S(1)}, u32[]{:S(2)}, u32[]{:S(2)}) collective-permute-start(f32[64,2176]{1,0:T(8,128)S(1)} %get-tuple-element.15), channel_id=1, source_target_pairs={{8,0},{16,8},{24,16},{32,24},{40,32},{48,40},{56,48},{64,56},{72,6... | collective-permute-start | bytes 1671176 | tf_op jit(solution)/shard_map/ppermute | solution.py:455
  7.4 2.5 %collective-permute-start.2 = (f32[8,2176]{1,0:T(8,128)S(1)}, f32[8,2176]{1,0:T(8,128)S(1)}, u32[]{:S(2)}, u32[]{:S(2)}) collective-permute-start(f32[8,2176]{1,0:T(8,128)S(1)} %get-tuple-element.16.own_last), channel_id=1, source_target_pairs={{0,1},{1,2},{2,3},{3,4},{4,5},{5,6},{6,7},{8,9},{9,10},{10,11},{11... | collective-permute-start | bytes 208904 | tf_op jit(solution)/shard_map/ppermute | solution.py:455
  9.9 1.3 %collective-permute-start.3 = (f32[8,2176]{1,0:T(8,128)S(1)}, f32[8,2176]{1,0:T(8,128)S(1)}, u32[]{:S(2)}, u32[]{:S(2)}) collective-permute-start(f32[8,2176]{1,0:T(8,128)S(1)} %get-tuple-element.17.own_first), channel_id=1, source_target_pairs={{1,0},{2,1},{3,2},{4,3},{5,4},{6,5},{7,6},{9,8},{10,9},{11,10},{12... | collective-permute-start | bytes 208904 | tf_op jit(solution)/shard_map/ppermute | solution.py:455
  11.2 0.0 copy-done.8
  11.2 0.0 copy-done.9
  11.3 0.0 copy-start
  11.3 0.0 copy-start.2
  11.3 0.0 copy-start.3
  11.3 0.0 copy-start.4
  11.3 0.0 copy-start.5
  11.3 0.0 copy-start.6
  11.3 0.0 copy-start.7
  11.3 14.3 %diode.1 = (f32[16,128,512]{2,1,0:T(8,128)S(1)}, f32[16,128,512]{2,1,0:T(8,128)S(1)}) custom-call(f32[8,64,2048]{2,1,0:T(8,128)S(1)} %get-tuple-element.11.volt_ref, bf16[256,256]{1,0:T(8,128)(2,1)S(1)} %copy-done.9, f32[128,1024]{1,0:T(8,128)S(1)} %copy-done.8), custom_call_target="tpu_custom_call" | custom-call | flops 4194304000 | bytes 4194304 | tf_op jit(solution)/shard_map/diode/pallas_call | solution.py:395
  25.6 0.0 collective-permute-done.2.col_low
  25.7 0.0 collective-permute-done.3.col_high
  25.7 0.0 collective-permute-done.row_low
  25.7 0.0 collective-permute-done.1.row_high
  25.7 0.0 copy-done
  25.7 0.0 copy-done.2
  25.7 0.0 copy-done.3
  25.7 0.0 copy-done.4
  25.7 0.0 copy-done.5
  25.7 0.0 copy-done.6
  25.7 0.0 copy-done.7
  25.8 7.6 %residual.1 = (f32[8,64,2048]{2,1,0:T(8,128)}, f32[32,128]{1,0:T(8,128)S(1)}) custom-call(f32[8]{0:T(128)S(1)} %copy-done.6, f32[8]{0:T(128)S(1)} %copy-done.7, f32[16,128,512]{2,1,0:T(8,128)S(1)} %get-tuple-element.12.turned, f32[16,128,512]{2,1,0:T(8,128)S(1)} %get-tuple-element.13.diode_ref, f32[8,64,2048]{2,1,0:T(8,128)S(1)} %copy-done, ...), custom_call_target="tpu_custom_call" | custom-call | flops 31457280 | bytes 8388608 | tf_op jit(solution)/shard_map/residual/pallas_call | solution.py:413
  33.4 19.3 %all_to_all.15 = f32[32,1,128]{2,1,0:T(1,128)S(1)} all-to-all(f32[32,1,128]{2,1,0:T(1,128)S(1)} %bitcast.9), channel_id=1, replica_groups=mesh['gx'=32,'gy'=8] {'gx'}, dimensions={0} | all-to-all | bytes 32768 | tf_op jit(solution)/shard_map/all_to_all | solution.py:459
  52.7 0.1 reduce_sum.18
  52.8 15.0 %all_to_all.16 = f32[8,1,128]{2,1,0:T(1,128)S(1)} all-to-all(f32[8,1,128]{2,1,0:T(1,128)S(1)} %broadcast_in_dim.3), channel_id=1, replica_groups=mesh['gx'=32,'gy'=8] {'gy'}, dimensions={0} | all-to-all | bytes 8192 | tf_op jit(solution)/shard_map/all_to_all | solution.py:459
  67.8 0.5 add_sqrt_fusion
  (2 shorter events, 0.0 us)
Async XLA Ops:
  0.6 0.9 %copy-start.1 = (s32[8,64,32]{1,2,0:T(8,128)S(1)}, s32[8,64,32]{1,2,0:T(8,128)}, u32[]{:S(2)}) copy-start(s32[8,64,32]{1,2,0:T(8,128)} %param.13) | copy-start | bytes 196612
  1.5 9.7 %copy-start.8 = (f32[128,1024]{1,0:T(8,128)S(1)}, f32[128,1024]{1,0:T(8,128)}, u32[]{:S(2)}) copy-start(f32[128,1024]{1,0:T(8,128)} %constant.18.clone.backward_ref) | copy-start | bytes 1572868
  1.5 9.7 %copy-start.9 = (bf16[256,256]{1,0:T(8,128)(2,1)S(1)}, bf16[256,256]{1,0:T(8,128)(2,1)}, u32[]{:S(2)}) copy-start(bf16[256,256]{1,0:T(8,128)(2,1)} %constant.17.clone.forward_ref) | copy-start | bytes 393220
  4.1 21.6 %collective-permute-start = (f32[64,2176]{1,0:T(8,128)S(1)}, f32[64,2176]{1,0:T(8,128)S(1)}, u32[]{:S(2)}, u32[]{:S(2)}) collective-permute-start(f32[64,2176]{1,0:T(8,128)S(1)} %get-tuple-element.14), channel_id=1, source_target_pairs={{0,8},{8,16},{16,24},{24,32},{32,40},{40,48},{48,56},{56,64},{64,7... | collective-permute-start | bytes 1671176 | tf_op jit(solution)/shard_map/ppermute | solution.py:455
  6.7 18.9 %collective-permute-start.1 = (f32[64,2176]{1,0:T(8,128)S(1)}, f32[64,2176]{1,0:T(8,128)S(1)}, u32[]{:S(2)}, u32[]{:S(2)}) collective-permute-start(f32[64,2176]{1,0:T(8,128)S(1)} %get-tuple-element.15), channel_id=1, source_target_pairs={{8,0},{16,8},{24,16},{32,24},{40,32},{48,40},{56,48},{64,56},{72,6... | collective-permute-start | bytes 1671176 | tf_op jit(solution)/shard_map/ppermute | solution.py:455
  7.4 18.2 %collective-permute-start.2 = (f32[8,2176]{1,0:T(8,128)S(1)}, f32[8,2176]{1,0:T(8,128)S(1)}, u32[]{:S(2)}, u32[]{:S(2)}) collective-permute-start(f32[8,2176]{1,0:T(8,128)S(1)} %get-tuple-element.16.own_last), channel_id=1, source_target_pairs={{0,1},{1,2},{2,3},{3,4},{4,5},{5,6},{6,7},{8,9},{9,10},{10,11},{11... | collective-permute-start | bytes 208904 | tf_op jit(solution)/shard_map/ppermute | solution.py:455
  9.9 15.7 %collective-permute-start.3 = (f32[8,2176]{1,0:T(8,128)S(1)}, f32[8,2176]{1,0:T(8,128)S(1)}, u32[]{:S(2)}, u32[]{:S(2)}) collective-permute-start(f32[8,2176]{1,0:T(8,128)S(1)} %get-tuple-element.17.own_first), channel_id=1, source_target_pairs={{1,0},{2,1},{3,2},{4,3},{5,4},{6,5},{7,6},{9,8},{10,9},{11,10},{12... | collective-permute-start | bytes 208904 | tf_op jit(solution)/shard_map/ppermute | solution.py:455
  11.3 14.4 %copy-start = (f32[8,64,2048]{2,1,0:T(8,128)S(1)}, f32[8,64,2048]{2,1,0:T(8,128)}, u32[]{:S(2)}) copy-start(f32[8,64,2048]{2,1,0:T(8,128)} %drive_ref.1) | copy-start | bytes 12582916
  11.3 14.4 %copy-start.2 = (bf16[96,2048]{1,0:T(8,128)(2,1)S(1)}, bf16[96,2048]{1,0:T(8,128)(2,1)}, u32[]{:S(2)}) copy-start(bf16[96,2048]{1,0:T(8,128)(2,1)} %constant.21.clone.widen_ref) | copy-start | bytes 1179652
  11.3 14.4 %copy-start.3 = (s32[8,64,32]{1,2,0:T(8,128)S(1)}, s32[8,64,32]{1,2,0:T(8,128)}, u32[]{:S(2)}) copy-start(s32[8,64,32]{1,2,0:T(8,128)} %param.14) | copy-start | bytes 196612
  11.3 14.4 %copy-start.4 = (f32[16,512]{1,0:T(8,128)S(1)}, f32[16,512]{1,0:T(8,128)}, u32[]{:S(2)}) copy-start(f32[16,512]{1,0:T(8,128)} %constant.20.clone.spread_ref) | copy-start | bytes 98308
  11.3 14.4 %copy-start.5 = (f32[64,128]{1,0:T(8,128)S(1)}, f32[64,128]{1,0:T(8,128)}, u32[]{:S(2)}) copy-start(f32[64,128]{1,0:T(8,128)} %constant.19.clone.rates_ref) | copy-start | bytes 98308
  11.3 14.4 %copy-start.6 = (f32[8]{0:T(128)S(1)}, f32[8]{0:T(128)}, u32[]{:S(2)}) copy-start(f32[8]{0:T(128)} %sigma_ref.1) | copy-start | bytes 100
  11.3 14.4 %copy-start.7 = (f32[8]{0:T(128)S(1)}, f32[8]{0:T(128)}, u32[]{:S(2)}) copy-start(f32[8]{0:T(128)} %cap_ref.1) | copy-start | bytes 100

commit v4 on v3

--- a/solution.py
+++ b/solution.py
@@ -187,7 +187,7 @@
     column = jnp.where(first, lane, lane - COLS)
     region = [beside(region_ref, g) for g in range(GROUPS)]
     conduct = [look_up(r, sigma_ref) for r in region]
-    row_kinds = jnp.concatenate([message[:, WIDTH:] for message in rows], axis=0).T
+    row_kinds = jnp.concatenate(rows, axis=0).T
     row_halo = look_up(row_kinds[:NZ] - 1.0, sigma_ref)
     outer = look_up(jnp.concatenate([kinds_of(m) for m in cols], axis=0), sigma_ref)
     inner = look_up(jnp.concatenate([kinds_of(m) for m in own_cols], axis=0), sigma_ref)
@@ -230,12 +230,12 @@
     drive_ref,
     region_ref,
     mask_ref,
-    row_low,
-    row_high,
-    col_low,
-    col_high,
-    own_first,
-    own_last,
+    row_near,
+    row_far,
+    col_near,
+    col_far,
+    own_near,
+    own_far,
     rates_ref,
     spread_ref,
     widen_ref,
@@ -246,15 +246,20 @@
     *scratch,
 ):
     sums, ready, sent = scratch[:2], scratch[2], scratch[3]
-    cols = [col_low[...], col_high[...]]
+    up, down = is_even("gx"), is_even("gy")
+
+    def low_high(even, near, far):
+        return [jnp.where(even, far, near), jnp.where(even, near, far)]
+
+    cols = low_high(down, col_near[...], col_far[...])
     rim = fill_factors(
         sigma_ref,
         cap_ref,
         region_ref,
         mask_ref,
-        [row_low, row_high],
+        low_high(up, row_near[:, WIDTH:], row_far[:, WIDTH:]),
         cols,
-        [own_first[...], own_last[...]],
+        low_high(down, own_near[...], own_far[...]),
         spread_ref[...],
         factors,
     )
@@ -268,7 +273,7 @@
 
     def gather(pair, slot):
         row_halo = jnp.concatenate(
-            [layers_of(row_low, pair)[...], layers_of(row_high, pair)[...]], axis=0
+            low_high(up, layers_of(row_near, pair)[...], layers_of(row_far, pair)[...]), axis=0
         ).T
         for half in range(2):
             layer = 2 * pair + half
@@ -346,8 +351,12 @@
     return [pl.BlockSpec(memory_space=pltpu.VMEM)] * count
 
 
+def is_even(axis):
+    return lax.rem(lax.axis_index(axis), 2) == 0
+
+
 def pack_kernel(volt_hbm, region_hbm, *refs):
-    row_first, row_last, col_first, col_last, volt_ref, region_ref, arrived = refs
+    row_near, row_far, col_near, col_far, volt_ref, region_ref, arrived = refs
     fetches = [
         pltpu.make_async_copy(volt_hbm.at[row], volt_ref.at[row], arrived.at[row])
         for row in range(ROWS)
@@ -356,8 +365,6 @@
     for fetch in reversed(fetches):
         fetch.start()
     fetches[ROWS].wait()
-    kinds = [region_ref[row].astype(jnp.float32).T + 1.0 for row in range(ROWS)]
-
     def put(message, volts, regions):
         message[:, :WIDTH] = volts
         padding = jnp.zeros((regions.shape[0], LANES - NZ), jnp.float32)
@@ -365,11 +372,22 @@
 
     for row in reversed(range(ROWS)):
         fetches[row].wait()
-    put(row_last, volt_ref[ROWS - 1], kinds[ROWS - 1])
-    put(row_first, volt_ref[0], kinds[0])
-    for message, col in ((col_first, 0), (col_last, COLS - 1)):
-        regions = jnp.concatenate([kind[col : col + 1] for kind in kinds], axis=0)
-        put(message, volt_ref[:, col, :], regions)
+    def kinds_at(row):
+        return region_ref[row].astype(jnp.float32).T + 1.0
+
+    kinds = [kinds_at(row) for row in range(ROWS)]
+    up, down = is_even("gx"), is_even("gy")
+    for message, row in (
+        (row_near, jnp.where(up, ROWS - 1, 0)),
+        (row_far, jnp.where(up, 0, ROWS - 1)),
+    ):
+        put(message, volt_ref[row], kinds_at(row))
+    sides = [
+        (volt_ref[:, col, :], jnp.concatenate([kind[col : col + 1] for kind in kinds], axis=0))
+        for col in (0, COLS - 1)
+    ]
+    for message, even, odd in ((col_near, sides[1], sides[0]), (col_far, sides[0], sides[1])):
+        put(message, *(jnp.where(down, e, o) for e, o in zip(even, odd)))
 
 
 def packed(volt, region):
@@ -446,13 +464,14 @@
     )
 
 
-def neighbours(first, last, axis, periodic):
+def swapped_halos(near, far, axis, periodic):
     count = lax.axis_size(axis)
-    forward = [(i, i + 1) for i in range(count - 1)]
+    close = [(i, i ^ 1) for i in range(count)]
+    apart = [(i, i + 1 if i % 2 else i - 1) for i in range(count)]
     if periodic:
-        forward.append((count - 1, 0))
-    backward = [(target, source) for source, target in forward]
-    return lax.ppermute(last, axis, forward), lax.ppermute(first, axis, backward)
+        apart = [(source, target % count) for source, target in apart]
+    apart = [(source, target) for source, target in apart if 0 <= target < count]
+    return lax.ppermute(near, axis, close), lax.ppermute(far, axis, apart)
 
 
 def exchanged_sum(copies, axis):
@@ -462,9 +481,9 @@
 def body(volt, drive, region, diode_mask, sigma_table, cap_table):
     by_layer = jnp.transpose(region, (0, 2, 1))
     mask = jnp.transpose(diode_mask, (0, 2, 1))
-    row_first, row_last, col_first, col_last, volt = packed(volt, by_layer)
-    rows = neighbours(row_first, row_last, "gx", True)
-    cols = neighbours(col_first, col_last, "gy", False)
+    row_near, row_far, col_near, col_far, volt = packed(volt, by_layer)
+    rows = swapped_halos(row_near, row_far, "gx", True)
+    cols = swapped_halos(col_near, col_far, "gy", False)
     turned, diode = diode_part(volt)
     nx, ny = lax.axis_size("gx"), lax.axis_size("gy")
     residual, squares = whole_residual(
@@ -474,7 +493,7 @@
         by_layer,
         mask,
         rows + cols,
-        (col_first, col_last),
+        (col_near, col_far),
         (sigma_table, cap_table),
         nx,
     )

time: 68.6 us -> 63.1 us (0.920)
  blocking collectives: 34.4 us -> 31.3 us
  starting transfers between devices: 7.15 us -> 4.73 us
    all_to_all x2, blocking collectives: 34.4 us -> 31.3 us  [exchanged_sum(): return jnp.sum(lax.all_to_all(copies, axis, 0, 0, tiled=True), axis=0)]
    ppermute x4, starting transfers between devices: 7.15 us -> 4.73 us  [swapped_halos(): return (lax.ppermute(near, axis, close), lax.ppermute(far, axis, apart))]
  transfers between devices with their start and end apart: 4 -> 4, of which waited for: 0 -> 0; matrix products, arithmetic and copies ran while one was open for 0% -> 0% of each run, Pallas kernels for 21% -> 23%
where the time goes in v4:
time: 63.1 us; the launch traced here: 62.9 us
  blocking collectives  31.3 us (50%)
  Pallas kernels  24.5 us (39%)
  starting transfers between devices  4.73 us (7%)
  local copies, waits for them, and re-layouts  0.96 us (2%)
  between operations  0.83 us (1%)
    all_to_all x2, blocking collectives, exchanged_sum(): return jnp.sum(lax.all_to_all(copies, axis, 0, 0, tiled=True), axis=0)  31.3 us
    pallas_call x1, Pallas kernels, diode_part(): pl.pallas_call(diode_kernel, in_specs=in_vmem(3), out_specs=in_vmem(2), o...  14.3 us
    pallas_call x1, Pallas kernels, whole_residual(): pl.pallas_call(residual_kernel, in_specs=[smem, smem] + in_vmem(14), out_...  7.57 us
    ppermute x4, starting transfers between devices, swapped_halos(): return (lax.ppermute(near, axis, close), lax.ppermute(far, axis, apart))  4.73 us
    pallas_call x1, Pallas kernels, packed(): pl.pallas_call(pack_kernel, in_specs=[pl.BlockSpec(memory_space=pltpu.HBM...  2.61 us
  transfers between devices with their start and end apart: 4, of which 0 were waited for; matrix products, arithmetic and copies ran while one was open for 0% of the time, Pallas kernels for 23%

profile of v4, /device:TPU:1, one launch (start us, length us, event | category | flops | bytes accessed | tf_op | source)
XLA Modules:
  0.0 62.9 jit_solution(11650560908841520842)
XLA Ops:
  0.6 0.0 copy-start.1
  0.6 0.9 %copy-done.1 = s32[8,64,32]{1,2,0:T(8,128)S(1)} copy-done((s32[8,64,32]{1,2,0:T(8,128)S(1)}, s32[8,64,32]{1,2,0:T(8,128)}, u32[]{:S(2)}) %copy-start.1) | copy-done | bytes 65560
  1.5 0.0 copy-start.8
  1.5 0.0 copy-start.9
  1.5 2.6 %pack.1 = (f32[64,2176]{1,0:T(8,128)S(1)}, f32[64,2176]{1,0:T(8,128)S(1)}, f32[8,2176]{1,0:T(8,128)S(1)}, f32[8,2176]{1,0:T(8,128)S(1)}, f32[8,64,2048]{2,1,0:T(8,128)S(1)}) custom-call(f32[8,64,2048]{2,1,0:T(8,128)} %volt_hbm.1, s32[8,32,64]{2,1,0:T(8,128)S(1)} %bitcast.6), custom_call_target="tpu_custom_call" | custom-call | tf_op jit(solution)/shard_map/pack/pallas_call | solution.py:395
  4.2 3.3 %collective-permute-start = (f32[64,2176]{1,0:T(8,128)S(1)}, f32[64,2176]{1,0:T(8,128)S(1)}, u32[]{:S(2)}, u32[]{:S(2)}) collective-permute-start(f32[64,2176]{1,0:T(8,128)S(1)} %get-tuple-element.14), channel_id=1, source_target_pairs={{0,8},{8,0},{16,24},{24,16},{32,40},{40,32},{48,56},{56,48},{64,72... | collective-permute-start | bytes 1671176 | tf_op jit(solution)/shard_map/ppermute | solution.py:474
  7.4 0.0 collective-permute-start.1
  7.4 0.8 %collective-permute-start.2 = (f32[8,2176]{1,0:T(8,128)S(1)}, f32[8,2176]{1,0:T(8,128)S(1)}, u32[]{:S(2)}, u32[]{:S(2)}) collective-permute-start(f32[8,2176]{1,0:T(8,128)S(1)} %get-tuple-element.16.own_near), channel_id=1, source_target_pairs={{0,1},{1,0},{2,3},{3,2},{4,5},{5,4},{6,7},{7,6},{8,9},{9,8},{10,11... | collective-permute-start | bytes 208904 | tf_op jit(solution)/shard_map/ppermute | solution.py:474
  8.2 0.7 %collective-permute-start.3 = (f32[8,2176]{1,0:T(8,128)S(1)}, f32[8,2176]{1,0:T(8,128)S(1)}, u32[]{:S(2)}, u32[]{:S(2)}) collective-permute-start(f32[8,2176]{1,0:T(8,128)S(1)} %get-tuple-element.17.own_far), channel_id=1, source_target_pairs={{1,2},{2,1},{3,4},{4,3},{5,6},{6,5},{9,10},{10,9},{11,12},{12,11},... | collective-permute-start | bytes 208904 | tf_op jit(solution)/shard_map/ppermute | solution.py:474
  8.9 0.0 copy-done.8
  8.9 0.0 copy-done.9
  8.9 0.0 copy-start
  8.9 0.0 copy-start.2
  8.9 0.0 copy-start.3
  9.0 0.0 copy-start.4
  9.0 0.0 copy-start.5
  9.0 0.0 copy-start.6
  9.0 0.0 copy-start.7
  9.0 14.3 %diode.1 = (f32[16,128,512]{2,1,0:T(8,128)S(1)}, f32[16,128,512]{2,1,0:T(8,128)S(1)}) custom-call(f32[8,64,2048]{2,1,0:T(8,128)S(1)} %get-tuple-element.11.volt_ref, bf16[256,256]{1,0:T(8,128)(2,1)S(1)} %copy-done.9, f32[128,1024]{1,0:T(8,128)S(1)} %copy-done.8), custom_call_target="tpu_custom_call" | custom-call | flops 4194304000 | bytes 4194304 | tf_op jit(solution)/shard_map/diode/pallas_call | solution.py:413
  23.3 0.0 collective-permute-done.2.col_near
  23.3 0.0 collective-permute-done.3.col_far
  23.3 0.0 collective-permute-done.row_near
  23.3 0.0 collective-permute-done.1.row_far
  23.3 0.0 copy-done
  23.4 0.0 copy-done.2
  23.4 0.0 copy-done.3
  23.4 0.0 copy-done.4
  23.4 0.0 copy-done.5
  23.4 0.0 copy-done.6
  23.4 0.0 copy-done.7
  23.4 7.6 %residual.1 = (f32[8,64,2048]{2,1,0:T(8,128)}, f32[32,128]{1,0:T(8,128)S(1)}) custom-call(f32[8]{0:T(128)S(1)} %copy-done.6, f32[8]{0:T(128)S(1)} %copy-done.7, f32[16,128,512]{2,1,0:T(8,128)S(1)} %get-tuple-element.12.turned, f32[16,128,512]{2,1,0:T(8,128)S(1)} %get-tuple-element.13.diode_ref, f32[8,64,2048]{2,1,0:T(8,128)S(1)} %copy-done, ...), custom_call_target="tpu_custom_call" | custom-call | flops 31457280 | bytes 8388608 | tf_op jit(solution)/shard_map/residual/pallas_call | solution.py:431
  31.0 17.0 %all_to_all.15 = f32[32,1,128]{2,1,0:T(1,128)S(1)} all-to-all(f32[32,1,128]{2,1,0:T(1,128)S(1)} %bitcast.9), channel_id=1, replica_groups=mesh['gx'=32,'gy'=8] {'gx'}, dimensions={0} | all-to-all | bytes 32768 | tf_op jit(solution)/shard_map/all_to_all | solution.py:478
  48.0 0.1 reduce_sum.18
  48.0 14.3 %all_to_all.16 = f32[8,1,128]{2,1,0:T(1,128)S(1)} all-to-all(f32[8,1,128]{2,1,0:T(1,128)S(1)} %broadcast_in_dim.3), channel_id=1, replica_groups=mesh['gx'=32,'gy'=8] {'gy'}, dimensions={0} | all-to-all | bytes 8192 | tf_op jit(solution)/shard_map/all_to_all | solution.py:478
  62.4 0.5 add_sqrt_fusion
  (2 shorter events, 0.0 us)
Async XLA Ops:
  0.6 0.9 %copy-start.1 = (s32[8,64,32]{1,2,0:T(8,128)S(1)}, s32[8,64,32]{1,2,0:T(8,128)}, u32[]{:S(2)}) copy-start(s32[8,64,32]{1,2,0:T(8,128)} %param.13) | copy-start | bytes 196612
  1.5 7.4 %copy-start.8 = (f32[128,1024]{1,0:T(8,128)S(1)}, f32[128,1024]{1,0:T(8,128)}, u32[]{:S(2)}) copy-start(f32[128,1024]{1,0:T(8,128)} %constant.18.clone.backward_ref) | copy-start | bytes 1572868
  1.5 7.4 %copy-start.9 = (bf16[256,256]{1,0:T(8,128)(2,1)S(1)}, bf16[256,256]{1,0:T(8,128)(2,1)}, u32[]{:S(2)}) copy-start(bf16[256,256]{1,0:T(8,128)(2,1)} %constant.17.clone.forward_ref) | copy-start | bytes 393220
  4.2 19.2 %collective-permute-start = (f32[64,2176]{1,0:T(8,128)S(1)}, f32[64,2176]{1,0:T(8,128)S(1)}, u32[]{:S(2)}, u32[]{:S(2)}) collective-permute-start(f32[64,2176]{1,0:T(8,128)S(1)} %get-tuple-element.14), channel_id=1, source_target_pairs={{0,8},{8,0},{16,24},{24,16},{32,40},{40,32},{48,56},{56,48},{64,72... | collective-permute-start | bytes 1671176 | tf_op jit(solution)/shard_map/ppermute | solution.py:474
  7.4 15.9 %collective-permute-start.1 = (f32[64,2176]{1,0:T(8,128)S(1)}, f32[64,2176]{1,0:T(8,128)S(1)}, u32[]{:S(2)}, u32[]{:S(2)}) collective-permute-start(f32[64,2176]{1,0:T(8,128)S(1)} %get-tuple-element.15), channel_id=1, source_target_pairs={{0,248},{8,16},{16,8},{24,32},{32,24},{40,48},{48,40},{56,64},{64,... | collective-permute-start | bytes 1671176 | tf_op jit(solution)/shard_map/ppermute | solution.py:474
  7.4 15.9 %collective-permute-start.2 = (f32[8,2176]{1,0:T(8,128)S(1)}, f32[8,2176]{1,0:T(8,128)S(1)}, u32[]{:S(2)}, u32[]{:S(2)}) collective-permute-start(f32[8,2176]{1,0:T(8,128)S(1)} %get-tuple-element.16.own_near), channel_id=1, source_target_pairs={{0,1},{1,0},{2,3},{3,2},{4,5},{5,4},{6,7},{7,6},{8,9},{9,8},{10,11... | collective-permute-start | bytes 208904 | tf_op jit(solution)/shard_map/ppermute | solution.py:474
  8.2 15.1 %collective-permute-start.3 = (f32[8,2176]{1,0:T(8,128)S(1)}, f32[8,2176]{1,0:T(8,128)S(1)}, u32[]{:S(2)}, u32[]{:S(2)}) collective-permute-start(f32[8,2176]{1,0:T(8,128)S(1)} %get-tuple-element.17.own_far), channel_id=1, source_target_pairs={{1,2},{2,1},{3,4},{4,3},{5,6},{6,5},{9,10},{10,9},{11,12},{12,11},... | collective-permute-start | bytes 208904 | tf_op jit(solution)/shard_map/ppermute | solution.py:474
  8.9 14.4 %copy-start = (f32[8,64,2048]{2,1,0:T(8,128)S(1)}, f32[8,64,2048]{2,1,0:T(8,128)}, u32[]{:S(2)}) copy-start(f32[8,64,2048]{2,1,0:T(8,128)} %drive_ref.1) | copy-start | bytes 12582916
  8.9 14.4 %copy-start.2 = (bf16[96,2048]{1,0:T(8,128)(2,1)S(1)}, bf16[96,2048]{1,0:T(8,128)(2,1)}, u32[]{:S(2)}) copy-start(bf16[96,2048]{1,0:T(8,128)(2,1)} %constant.21.clone.widen_ref) | copy-start | bytes 1179652
  8.9 14.4 %copy-start.3 = (s32[8,64,32]{1,2,0:T(8,128)S(1)}, s32[8,64,32]{1,2,0:T(8,128)}, u32[]{:S(2)}) copy-start(s32[8,64,32]{1,2,0:T(8,128)} %param.14) | copy-start | bytes 196612
  9.0 14.4 %copy-start.4 = (f32[16,512]{1,0:T(8,128)S(1)}, f32[16,512]{1,0:T(8,128)}, u32[]{:S(2)}) copy-start(f32[16,512]{1,0:T(8,128)} %constant.20.clone.spread_ref) | copy-start | bytes 98308
  9.0 14.4 %copy-start.5 = (f32[64,128]{1,0:T(8,128)S(1)}, f32[64,128]{1,0:T(8,128)}, u32[]{:S(2)}) copy-start(f32[64,128]{1,0:T(8,128)} %constant.19.clone.rates_ref) | copy-start | bytes 98308
  9.0 14.4 %copy-start.6 = (f32[8]{0:T(128)S(1)}, f32[8]{0:T(128)}, u32[]{:S(2)}) copy-start(f32[8]{0:T(128)} %sigma_ref.1) | copy-start | bytes 100
  9.0 14.4 %copy-start.7 = (f32[8]{0:T(128)S(1)}, f32[8]{0:T(128)}, u32[]{:S(2)}) copy-start(f32[8]{0:T(128)} %cap_ref.1) | copy-start | bytes 100

commit v5 on v4

--- a/solution.py
+++ b/solution.py
@@ -35,8 +35,8 @@
 GSUM = DIO + GROUPS
 FIELDS = GSUM + GROUPS
 
-UNROLL = 2
-PACK_MIB = 46
+UNROLL = 4
+PACK_MIB = 8
 
 CHUNK = 64
 
@@ -355,59 +355,66 @@
     return lax.rem(lax.axis_index(axis), 2) == 0
 
 
-def pack_kernel(volt_hbm, region_hbm, *refs):
-    row_near, row_far, col_near, col_far, volt_ref, region_ref, arrived = refs
+def pack_kernel(volt_hbm, region_hbm, table_hbm, *refs):
+    row_near, row_far, col_near, col_far, table_ref, sides_ref, region_ref, arrived = refs
+    up, down = is_even("gx"), is_even("gy")
+    near_row = jnp.where(up, ROWS - 1, 0)
+    far_row = ROWS - 1 - near_row
     fetches = [
-        pltpu.make_async_copy(volt_hbm.at[row], volt_ref.at[row], arrived.at[row])
-        for row in range(ROWS)
+        pltpu.make_async_copy(region_hbm, region_ref, arrived.at[0]),
+        pltpu.make_async_copy(volt_hbm.at[:, 0], sides_ref.at[0], arrived.at[1]),
+        pltpu.make_async_copy(volt_hbm.at[:, COLS - 1], sides_ref.at[1], arrived.at[2]),
+        pltpu.make_async_copy(
+            volt_hbm.at[near_row], row_near.at[:, pl.ds(0, WIDTH)], arrived.at[3]
+        ),
+        pltpu.make_async_copy(volt_hbm.at[far_row], row_far.at[:, pl.ds(0, WIDTH)], arrived.at[4]),
+        pltpu.make_async_copy(table_hbm, table_ref, arrived.at[5]),
     ]
-    fetches.append(pltpu.make_async_copy(region_hbm, region_ref, arrived.at[ROWS]))
-    for fetch in reversed(fetches):
+    for fetch in fetches:
         fetch.start()
-    fetches[ROWS].wait()
-    def put(message, volts, regions):
-        message[:, :WIDTH] = volts
+    fetches[0].wait()
+
+    def kinds_at(row):
+        return region_ref[row].astype(jnp.float32).T + 1.0
+
+    def put_kinds(message, regions):
         padding = jnp.zeros((regions.shape[0], LANES - NZ), jnp.float32)
         message[:, WIDTH:] = jnp.concatenate([regions, padding], axis=1)
 
-    for row in reversed(range(ROWS)):
-        fetches[row].wait()
-    def kinds_at(row):
-        return region_ref[row].astype(jnp.float32).T + 1.0
-
     kinds = [kinds_at(row) for row in range(ROWS)]
-    up, down = is_even("gx"), is_even("gy")
-    for message, row in (
-        (row_near, jnp.where(up, ROWS - 1, 0)),
-        (row_far, jnp.where(up, 0, ROWS - 1)),
-    ):
-        put(message, volt_ref[row], kinds_at(row))
-    sides = [
-        (volt_ref[:, col, :], jnp.concatenate([kind[col : col + 1] for kind in kinds], axis=0))
-        for col in (0, COLS - 1)
+    put_kinds(row_near, kinds_at(near_row))
+    put_kinds(row_far, kinds_at(far_row))
+    low, high = [
+        jnp.concatenate([kind[col : col + 1] for kind in kinds], axis=0) for col in (0, COLS - 1)
     ]
-    for message, even, odd in ((col_near, sides[1], sides[0]), (col_far, sides[0], sides[1])):
-        put(message, *(jnp.where(down, e, o) for e, o in zip(even, odd)))
-
-
-def packed(volt, region):
-    shapes = [(COLS, WIDTH + LANES)] * 2 + [(ROWS, WIDTH + LANES)] * 2 + [volt.shape]
+    put_kinds(col_near, jnp.where(down, high, low))
+    put_kinds(col_far, jnp.where(down, low, high))
+    for fetch in fetches[1:]:
+        fetch.wait()
+    low, high = sides_ref[0], sides_ref[1]
+    col_near[:, :WIDTH] = jnp.where(down, high, low)
+    col_far[:, :WIDTH] = jnp.where(down, low, high)
+
+
+def packed(volt, region, table):
+    shapes = [(COLS, WIDTH + LANES)] * 2 + [(ROWS, WIDTH + LANES)] * 2 + [table.shape]
     return pl.pallas_call(
         pack_kernel,
-        in_specs=[pl.BlockSpec(memory_space=pltpu.HBM)] * 2,
+        in_specs=[pl.BlockSpec(memory_space=pltpu.HBM)] * 3,
         out_specs=in_vmem(5),
         out_shape=[jax.ShapeDtypeStruct(shape, jnp.float32) for shape in shapes],
         scratch_shapes=[
+            pltpu.VMEM((2, ROWS, WIDTH), jnp.float32),
             pltpu.VMEM(region.shape, region.dtype),
-            pltpu.SemaphoreType.DMA((ROWS + 1,)),
+            pltpu.SemaphoreType.DMA((6,)),
         ],
         compiler_params=pltpu.CompilerParams(vmem_limit_bytes=PACK_MIB * 1024 * 1024),
         name="pack",
-    )(volt, region)
-
-
-def diode_part(volt):
-    forward, backward = constant_tables()[:2]
+    )(*(pltpu.with_memory_space_constraint(array, pltpu.HBM) for array in (volt, region, table)))
+
+
+def diode_part(volt, backward):
+    forward = constant_tables()[0]
     samples = CELLS * NZ * S
     whole = jax.ShapeDtypeStruct((PAIRS, LANES, CELLS), jnp.float32)
     return pl.pallas_call(
@@ -422,7 +429,7 @@
             flops=samples * 1000, bytes_accessed=4 * CELLS * WIDTH, transcendentals=2 * samples
         ),
         name="diode",
-    )(volt, jnp.asarray(forward), jnp.asarray(backward))
+    )(volt, jnp.asarray(forward), backward)
 
 
 def whole_residual(turned, diode, drive, region, mask, halos, own_cols, tables, copies):
@@ -481,10 +488,11 @@
 def body(volt, drive, region, diode_mask, sigma_table, cap_table):
     by_layer = jnp.transpose(region, (0, 2, 1))
     mask = jnp.transpose(diode_mask, (0, 2, 1))
-    row_near, row_far, col_near, col_far, volt = packed(volt, by_layer)
+    backward = jnp.asarray(constant_tables()[1])
+    row_near, row_far, col_near, col_far, backward = packed(volt, by_layer, backward)
     rows = swapped_halos(row_near, row_far, "gx", True)
     cols = swapped_halos(col_near, col_far, "gy", False)
-    turned, diode = diode_part(volt)
+    turned, diode = diode_part(volt, backward)
     nx, ny = lax.axis_size("gx"), lax.axis_size("gy")
     residual, squares = whole_residual(
         turned,

time: 63.1 us -> 60.6 us (0.960)
  Pallas kernels: 24.5 us -> 22.9 us
  local copies, waits for them, and re-layouts: 0.96 us -> 0.07 us
    pallas_call x1, Pallas kernels: 2.61 us -> 1.72 us  [packed(): pl.pallas_call(pack_kernel, in_specs=[pl.BlockSpec(memory_space=pltpu.HBM...]
    unnamed x20, local copies, waits for them, and re-layouts: 0.95 us -> 0.06 us
    pallas_call x1, Pallas kernels: 14.3 us -> 13.7 us  [diode_part(): pl.pallas_call(diode_kernel, in_specs=in_vmem(3), out_specs=in_vmem(2), o...]
where the time goes in v5:
time: 60.6 us; the launch traced here: 60.5 us
  blocking collectives  31.3 us (52%)
  Pallas kernels  22.9 us (38%)
  starting transfers between devices  4.73 us (8%)
  between operations  0.85 us (1%)
    all_to_all x2, blocking collectives, exchanged_sum(): return jnp.sum(lax.all_to_all(copies, axis, 0, 0, tiled=True), axis=0)  31.3 us
    pallas_call x1, Pallas kernels, diode_part(): pl.pallas_call(diode_kernel, in_specs=in_vmem(3), out_specs=in_vmem(2), o...  13.7 us
    pallas_call x1, Pallas kernels, whole_residual(): pl.pallas_call(residual_kernel, in_specs=[smem, smem] + in_vmem(14), out_...  7.56 us
    ppermute x4, starting transfers between devices, swapped_halos(): return (lax.ppermute(near, axis, close), lax.ppermute(far, axis, apart))  4.73 us
    pallas_call x1, Pallas kernels, packed(): pl.pallas_call(pack_kernel, in_specs=[pl.BlockSpec(memory_space=pltpu.HBM...  1.72 us
  transfers between devices with their start and end apart: 4, of which 0 were waited for; matrix products, arithmetic and copies ran while one was open for 0% of the time, Pallas kernels for 23%

profile of v5, /device:TPU:1, one launch (start us, length us, event | category | flops | bytes accessed | tf_op | source)
XLA Modules:
  0.0 60.5 jit_solution(8467614608967385626)
XLA Ops:
  0.6 0.0 copy-start.9
  0.6 0.0 copy-start.1
  0.7 1.7 %pack.1 = (f32[64,2176]{1,0:T(8,128)S(1)}, f32[64,2176]{1,0:T(8,128)S(1)}, f32[8,2176]{1,0:T(8,128)S(1)}, f32[8,2176]{1,0:T(8,128)S(1)}, f32[128,1024]{1,0:T(8,128)S(1)}) custom-call(f32[8,64,2048]{2,1,0:T(8,128)} %volt_ref.1, s32[8,32,64]{2,1,0:T(8,128)} %bitcast.6, f32[128,1024]{1,0:T(8,128)} %constant.17.clone.table_hbm), custom_call_target="tpu_custom_call" | custom-call | tf_op jit(solution)/shard_map/pack/pallas_call | solution.py:401
  2.4 3.3 %collective-permute-start = (f32[64,2176]{1,0:T(8,128)S(1)}, f32[64,2176]{1,0:T(8,128)S(1)}, u32[]{:S(2)}, u32[]{:S(2)}) collective-permute-start(f32[64,2176]{1,0:T(8,128)S(1)} %get-tuple-element.14), channel_id=1, source_target_pairs={{0,8},{8,0},{16,24},{24,16},{32,40},{40,32},{48,56},{56,48},{64,72... | collective-permute-start | bytes 1671176 | tf_op jit(solution)/shard_map/ppermute | solution.py:481
  5.7 0.0 collective-permute-start.1
  5.7 0.8 %collective-permute-start.2 = (f32[8,2176]{1,0:T(8,128)S(1)}, f32[8,2176]{1,0:T(8,128)S(1)}, u32[]{:S(2)}, u32[]{:S(2)}) collective-permute-start(f32[8,2176]{1,0:T(8,128)S(1)} %get-tuple-element.16.own_near), channel_id=1, source_target_pairs={{0,1},{1,0},{2,3},{3,2},{4,5},{5,4},{6,7},{7,6},{8,9},{9,8},{10,11... | collective-permute-start | bytes 208904 | tf_op jit(solution)/shard_map/ppermute | solution.py:481
  6.4 0.7 %collective-permute-start.3 = (f32[8,2176]{1,0:T(8,128)S(1)}, f32[8,2176]{1,0:T(8,128)S(1)}, u32[]{:S(2)}, u32[]{:S(2)}) collective-permute-start(f32[8,2176]{1,0:T(8,128)S(1)} %get-tuple-element.17.own_far), channel_id=1, source_target_pairs={{1,2},{2,1},{3,4},{4,3},{5,6},{6,5},{9,10},{10,9},{11,12},{12,11},... | collective-permute-start | bytes 208904 | tf_op jit(solution)/shard_map/ppermute | solution.py:481
  7.1 0.0 copy-done.9
  7.1 0.0 copy-done.1
  7.1 0.0 copy-start
  7.1 0.0 copy-start.2
  7.2 0.0 copy-start.3
  7.2 0.0 copy-start.4
  7.2 0.0 copy-start.5
  7.2 0.0 copy-start.6
  7.2 0.0 copy-start.7
  7.2 0.0 copy-start.8
  7.2 13.7 %diode.1 = (f32[16,128,512]{2,1,0:T(8,128)S(1)}, f32[16,128,512]{2,1,0:T(8,128)S(1)}) custom-call(f32[8,64,2048]{2,1,0:T(8,128)S(1)} %copy-done.1, bf16[256,256]{1,0:T(8,128)(2,1)S(1)} %copy-done.9, f32[128,1024]{1,0:T(8,128)S(1)} %get-tuple-element.11.backward_ref), custom_call_target="tpu_custom_call" | custom-call | flops 4194304000 | bytes 4194304 | tf_op jit(solution)/shard_map/diode/pallas_call | solution.py:420
  20.9 0.0 collective-permute-done.2.col_near
  20.9 0.0 collective-permute-done.3.col_far
  20.9 0.0 collective-permute-done.row_near
  20.9 0.0 collective-permute-done.1.row_far
  20.9 0.0 copy-done
  20.9 0.0 copy-done.2
  21.0 0.0 copy-done.3
  21.0 0.0 copy-done.4
  21.0 0.0 copy-done.5
  21.0 0.0 copy-done.6
  21.0 0.0 copy-done.7
  21.0 0.0 copy-done.8
  21.0 7.6 %residual.1 = (f32[8,64,2048]{2,1,0:T(8,128)}, f32[32,128]{1,0:T(8,128)S(1)}) custom-call(f32[8]{0:T(128)S(1)} %copy-done.7, f32[8]{0:T(128)S(1)} %copy-done.8, f32[16,128,512]{2,1,0:T(8,128)S(1)} %get-tuple-element.12.turned, f32[16,128,512]{2,1,0:T(8,128)S(1)} %get-tuple-element.13.diode_ref, f32[8,64,2048]{2,1,0:T(8,128)S(1)} %copy-done, ...), custom_call_target="tpu_custom_call" | custom-call | flops 31457280 | bytes 8388608 | tf_op jit(solution)/shard_map/residual/pallas_call | solution.py:438
  28.6 17.0 %all_to_all.15 = f32[32,1,128]{2,1,0:T(1,128)S(1)} all-to-all(f32[32,1,128]{2,1,0:T(1,128)S(1)} %bitcast.9), channel_id=1, replica_groups=mesh['gx'=32,'gy'=8] {'gx'}, dimensions={0} | all-to-all | bytes 32768 | tf_op jit(solution)/shard_map/all_to_all | solution.py:485
  45.6 0.1 reduce_sum.18
  45.6 14.3 %all_to_all.16 = f32[8,1,128]{2,1,0:T(1,128)S(1)} all-to-all(f32[8,1,128]{2,1,0:T(1,128)S(1)} %broadcast_in_dim.3), channel_id=1, replica_groups=mesh['gx'=32,'gy'=8] {'gy'}, dimensions={0} | all-to-all | bytes 8192 | tf_op jit(solution)/shard_map/all_to_all | solution.py:485
  59.9 0.5 add_sqrt_fusion
  (2 shorter events, 0.0 us)
Async XLA Ops:
  0.6 6.5 %copy-start.9 = (bf16[256,256]{1,0:T(8,128)(2,1)S(1)}, bf16[256,256]{1,0:T(8,128)(2,1)}, u32[]{:S(2)}) copy-start(bf16[256,256]{1,0:T(8,128)(2,1)} %constant.18.clone.forward_ref) | copy-start | bytes 393220
  0.6 6.5 %copy-start.1 = (f32[8,64,2048]{2,1,0:T(8,128)S(1)}, f32[8,64,2048]{2,1,0:T(8,128)}, u32[]{:S(2)}) copy-start(f32[8,64,2048]{2,1,0:T(8,128)} %volt_ref.1) | copy-start | bytes 12582916
  2.4 18.5 %collective-permute-start = (f32[64,2176]{1,0:T(8,128)S(1)}, f32[64,2176]{1,0:T(8,128)S(1)}, u32[]{:S(2)}, u32[]{:S(2)}) collective-permute-start(f32[64,2176]{1,0:T(8,128)S(1)} %get-tuple-element.14), channel_id=1, source_target_pairs={{0,8},{8,0},{16,24},{24,16},{32,40},{40,32},{48,56},{56,48},{64,72... | collective-permute-start | bytes 1671176 | tf_op jit(solution)/shard_map/ppermute | solution.py:481
  5.7 15.3 %collective-permute-start.1 = (f32[64,2176]{1,0:T(8,128)S(1)}, f32[64,2176]{1,0:T(8,128)S(1)}, u32[]{:S(2)}, u32[]{:S(2)}) collective-permute-start(f32[64,2176]{1,0:T(8,128)S(1)} %get-tuple-element.15), channel_id=1, source_target_pairs={{0,248},{8,16},{16,8},{24,32},{32,24},{40,48},{48,40},{56,64},{64,... | collective-permute-start | bytes 1671176 | tf_op jit(solution)/shard_map/ppermute | solution.py:481
  5.7 15.2 %collective-permute-start.2 = (f32[8,2176]{1,0:T(8,128)S(1)}, f32[8,2176]{1,0:T(8,128)S(1)}, u32[]{:S(2)}, u32[]{:S(2)}) collective-permute-start(f32[8,2176]{1,0:T(8,128)S(1)} %get-tuple-element.16.own_near), channel_id=1, source_target_pairs={{0,1},{1,0},{2,3},{3,2},{4,5},{5,4},{6,7},{7,6},{8,9},{9,8},{10,11... | collective-permute-start | bytes 208904 | tf_op jit(solution)/shard_map/ppermute | solution.py:481
  6.4 14.5 %collective-permute-start.3 = (f32[8,2176]{1,0:T(8,128)S(1)}, f32[8,2176]{1,0:T(8,128)S(1)}, u32[]{:S(2)}, u32[]{:S(2)}) collective-permute-start(f32[8,2176]{1,0:T(8,128)S(1)} %get-tuple-element.17.own_far), channel_id=1, source_target_pairs={{1,2},{2,1},{3,4},{4,3},{5,6},{6,5},{9,10},{10,9},{11,12},{12,11},... | collective-permute-start | bytes 208904 | tf_op jit(solution)/shard_map/ppermute | solution.py:481
  7.1 13.8 %copy-start = (f32[8,64,2048]{2,1,0:T(8,128)S(1)}, f32[8,64,2048]{2,1,0:T(8,128)}, u32[]{:S(2)}) copy-start(f32[8,64,2048]{2,1,0:T(8,128)} %drive_ref.1) | copy-start | bytes 12582916
  7.1 13.8 %copy-start.2 = (s32[8,64,32]{1,2,0:T(8,128)S(1)}, s32[8,64,32]{1,2,0:T(8,128)}, u32[]{:S(2)}) copy-start(s32[8,64,32]{1,2,0:T(8,128)} %param.13) | copy-start | bytes 196612
  7.2 13.8 %copy-start.3 = (bf16[96,2048]{1,0:T(8,128)(2,1)S(1)}, bf16[96,2048]{1,0:T(8,128)(2,1)}, u32[]{:S(2)}) copy-start(bf16[96,2048]{1,0:T(8,128)(2,1)} %constant.21.clone.widen_ref) | copy-start | bytes 1179652
  7.2 13.8 %copy-start.4 = (s32[8,64,32]{1,2,0:T(8,128)S(1)}, s32[8,64,32]{1,2,0:T(8,128)}, u32[]{:S(2)}) copy-start(s32[8,64,32]{1,2,0:T(8,128)} %param.14) | copy-start | bytes 196612
  7.2 13.8 %copy-start.5 = (f32[16,512]{1,0:T(8,128)S(1)}, f32[16,512]{1,0:T(8,128)}, u32[]{:S(2)}) copy-start(f32[16,512]{1,0:T(8,128)} %constant.20.clone.spread_ref) | copy-start | bytes 98308
  7.2 13.8 %copy-start.6 = (f32[64,128]{1,0:T(8,128)S(1)}, f32[64,128]{1,0:T(8,128)}, u32[]{:S(2)}) copy-start(f32[64,128]{1,0:T(8,128)} %constant.19.clone.rates_ref) | copy-start | bytes 98308
  7.2 13.8 %copy-start.7 = (f32[8]{0:T(128)S(1)}, f32[8]{0:T(128)}, u32[]{:S(2)}) copy-start(f32[8]{0:T(128)} %sigma_ref.1) | copy-start | bytes 100
  7.2 13.8 %copy-start.8 = (f32[8]{0:T(128)S(1)}, f32[8]{0:T(128)}, u32[]{:S(2)}) copy-start(f32[8]{0:T(128)} %cap_ref.1) | copy-start | bytes 100
